TPU v7x, 32 devices: a 4x4x1 block of a 4x4x8 slice. The times are simulated.
32 devices in a mesh: data: 1 (over z), tp: 32 (over y, x, core).
Axes of the slice: x: 4, y: 4, z: 1, core: 2. Of those that a mesh axis runs over, the one named last changes fastest.
The devices are a block of a 4x4x8 slice.
Arguments:
- x_tokens: bfloat16 [8192, 2560], P(('data', 'tp'))
- ln_gamma: float32 [2560], replicated
- w_qkv: bfloat16 [2560, 32, 240], P(None, 'tp')
- w_out: bfloat16 [32, 80, 2560], P('tp')
- w_up: bfloat16 [2560, 10240], P(None, 'tp')
- w_down: bfloat16 [10240, 2560], P('tp')
Outputs:
- output: bfloat16 [8192, 2560], P(('data', 'tp'))
All inputs are finite; a program needn't handle non-finite values.
Results may differ from a plain program's by a relative error of at most 0.00250589.
Values are sent between devices in bfloat16 or wider.
A program may use at most 768 MiB of HBM per device.

v0:
```python
import math
import jax
import jax.numpy as jnp
from jax import lax
from jax.sharding import PartitionSpec as P

LN_EPS = 1e-6


def layer_norm(row_vals, ln_gain):
    row_mean = jnp.mean(row_vals, axis=-1, keepdims=True)
    centered = row_vals - row_mean
    row_var = jnp.mean(centered * centered, axis=-1, keepdims=True)
    return (centered * lax.rsqrt(row_var + LN_EPS) * ln_gain).astype(jnp.bfloat16)


def block_rows(row_count, head_count):
    return min(row_count, 2 ** int(math.log2(max(8, 4096 // head_count))))


def attend(query_rows, key_rows, value_rows):
    row_count, head_count, head_dim = query_rows.shape
    q_size = block_rows(row_count, head_count)
    attn_scale = head_dim ** -0.5

    def one_block(query_blk):
        scores = jnp.einsum("qhe,khe->hqk", query_blk, key_rows, preferred_element_type=jnp.float32) * attn_scale
        row_max = jnp.max(scores, axis=-1, keepdims=True)
        exp_scores = jnp.exp(scores - row_max)
        exp_sum = jnp.sum(exp_scores, axis=-1, keepdims=True)
        block_out = jnp.einsum("hqk,khe->hqe", exp_scores.astype(jnp.bfloat16), value_rows, preferred_element_type=jnp.float32)
        return (block_out / exp_sum).astype(jnp.bfloat16)

    return lax.map(one_block, query_rows.reshape(row_count // q_size, q_size, head_count, head_dim))


def solution(mesh):
    def local_block(x_loc, ln_gamma, w_qkv, w_out, w_up, w_down):
        model_dim = x_loc.shape[1]
        head_dim = w_qkv.shape[2] // 3
        residual = x_loc.astype(jnp.float32)
        normed = layer_norm(residual, ln_gamma)
        gathered = lax.all_gather(normed, "tp", axis=0, tiled=True)
        seq_len = gathered.shape[0]
        qkv_rows = jnp.einsum("sd,dhc->shc", gathered, w_qkv, preferred_element_type=jnp.float32).astype(jnp.bfloat16)
        head_out = attend(qkv_rows[:, :, :head_dim], qkv_rows[:, :, head_dim:2 * head_dim], qkv_rows[:, :, 2 * head_dim:])
        attn_part = jnp.einsum("nhqe,hed->nqd", head_out, w_out, preferred_element_type=jnp.float32).reshape(seq_len, model_dim)
        pre_act = jnp.dot(gathered, w_up, preferred_element_type=jnp.float32)
        hidden = jax.nn.gelu(pre_act, approximate=True).astype(jnp.bfloat16)
        part_sum = attn_part + jnp.dot(hidden, w_down, preferred_element_type=jnp.float32)
        reduced = lax.psum_scatter(part_sum, "tp", scatter_dimension=0, tiled=True)
        return (residual + reduced).astype(jnp.bfloat16)

    row_spec = P(("data", "tp"), None)
    return jax.shard_map(local_block, mesh=mesh, in_specs=(row_spec, P(None), P(None, "tp", None), P("tp", None, None), P(None, "tp"), P("tp", None)), out_specs=row_spec, check_vma=False)
```

profile of v0, /device:TPU:97, one launch (start us, length us, event | category | flops | bytes accessed | tf_op | source)
XLA Modules:
  0.0 890.2 jit_solution(14506327810510881192)
XLA Ops:
  6.6 1.7 convert_reduce_fusion
  8.3 1.8 fusion.40
  10.1 1.5 fusion.42
  11.6 0.1 all-gather.2.cloned.1.call-update
  11.7 0.1 reduce-scatter.2.cloned.1.call-start
  11.8 134.7 %all-gather.2.cloned.1.call-done = bf16[8192,2560]{1,0:T(8,128)(2,1)} async-done(((bf16[256,2560]{1,0:T(8,128)(2,1)}), bf16[8192,2560]{1,0:T(8,128)(2,1)}) %all-gather.2.cloned.1.call-update) | async-done | bytes 41943056 | tf_op jit(solution)/shard_map/all_gather | solution.py:43
  146.5 20.2 %fusion.31 = bf16[8192,1,240]{0,2,1:T(8,128)(2,1)} fusion(bf16[8192,2560]{1,0:T(8,128)(2,1)} %all-gather.2.cloned.1.call-done, bf16[2560,1,240]{0,2,1:T(8,128)(2,1)} %param.10), kind=kOutput, calls=%fused_computation.27 | convolution fusion | flops 10068295680 | bytes 47104000 | tf_op jit(solution)/shard_map/sd,dhc->shc/dot_general | solution.py:45
  166.7 3.5 fusion.50
  170.2 1.2 copy.15
  171.4 263.0 %while.10 = (s32[]{:T(128)}, bf16[2,1,4096,80]{2,3,1,0:T(8,128)(2,1)}, bf16[2,4096,1,80]{1,3,2,0:T(8,128)(2,1)}, bf16[8192,1,80]{0,2,1:T(8,128)(2,1)S(1)}, bf16[8192,1,80]{0,2,1:T(8,128)(2,1)}, /*index=5*/s32[]{:T(128)}) while((s32[]{:T(128)}, bf16[2,1,4096,80]{2,3,1,0:T(8,128)(2,1)}, bf16[2,4096,1,80]{1,3,2,0:T(8,128)(2,1)}, ...), condition=%wide.region_5.6_spmd, body=%wide.region_2.5_spmd.sunk | while | flops 11006500864 | bytes 406668352 | solution.py:34
  171.4 46.1 %multiply_reduce_fusion.2 = (f32[4096]{0:T(1024)S(1)}, f32[4096,8192]{1,0:T(8,128)}) fusion(bf16[8192,1,80]{0,2,1:T(8,128)(2,1)S(1)} %get-tuple-element.108, bf16[2,4096,1,80]{1,3,2,0:T(8,128)(2,1)} %get-tuple-element.107, s32[]{:T(128)} %get-tuple-element.99), kind=kOutput, calls=%fused_computation.1.clone.2 | convolution fusion | flops 5435813888 | bytes 136200704 | tf_op jit(solution)/shard_map/while/body/eval_jaxpr/qhe,khe->hqk/dot_general | solution.py:27
  217.5 41.0 %fusion.71 = f32[4096]{0:T(1024)S(1)} fusion(f32[4096,8192]{1,0:T(8,128)} %get-tuple-element.91, f32[4096]{0:T(1024)S(1)} %get-tuple-element.92), kind=kLoop, calls=%fused_computation.2.clone.1 | loop fusion | flops 100659200 | bytes 134250496 | tf_op jit(solution)/shard_map/while/body/eval_jaxpr/reduce_sum | solution.py:30
  258.5 44.4 %fusion.72 = bf16[2,1,4096,80]{2,3,1,0:T(8,128)(2,1)} fusion(bf16[2,1,4096,80]{2,3,1,0:T(8,128)(2,1)} %get-tuple-element.100, s32[]{:T(128)} %get-tuple-element.99, f32[4096,8192]{1,0:T(8,128)} %get-tuple-element.91, f32[4096]{0:T(1024)S(1)} %get-tuple-element.92, bf16[8192,1,80]{0,2,1:T(8,128)(2,1)} %get-tuple-element.109, f32[4096]{0:T(1024)S(1)} %fusion.71), kind=kOutput, calls=%fused_computation.8.clone.1 | convolution fusion | flops 5470027776 | bytes 136217088 | tf_op jit(solution)/shard_map/while/body/eval_jaxpr/hqk,khe->hqe/dot_general | solution.py:31
  302.9 46.1 %multiply_reduce_fusion.2 = (f32[4096]{0:T(1024)S(1)}, f32[4096,8192]{1,0:T(8,128)}) fusion(bf16[8192,1,80]{0,2,1:T(8,128)(2,1)S(1)} %get-tuple-element.108, bf16[2,4096,1,80]{1,3,2,0:T(8,128)(2,1)} %get-tuple-element.107, s32[]{:T(128)} %get-tuple-element.99), kind=kOutput, calls=%fused_computation.1.clone.2 | convolution fusion | flops 5435813888 | bytes 136200704 | tf_op jit(solution)/shard_map/while/body/eval_jaxpr/qhe,khe->hqk/dot_general | solution.py:27
  349.0 41.0 %fusion.71 = f32[4096]{0:T(1024)S(1)} fusion(f32[4096,8192]{1,0:T(8,128)} %get-tuple-element.91, f32[4096]{0:T(1024)S(1)} %get-tuple-element.92), kind=kLoop, calls=%fused_computation.2.clone.1 | loop fusion | flops 100659200 | bytes 134250496 | tf_op jit(solution)/shard_map/while/body/eval_jaxpr/reduce_sum | solution.py:30
  390.1 44.4 %fusion.72 = bf16[2,1,4096,80]{2,3,1,0:T(8,128)(2,1)} fusion(bf16[2,1,4096,80]{2,3,1,0:T(8,128)(2,1)} %get-tuple-element.100, s32[]{:T(128)} %get-tuple-element.99, f32[4096,8192]{1,0:T(8,128)} %get-tuple-element.91, f32[4096]{0:T(1024)S(1)} %get-tuple-element.92, bf16[8192,1,80]{0,2,1:T(8,128)(2,1)} %get-tuple-element.109, f32[4096]{0:T(1024)S(1)} %fusion.71), kind=kOutput, calls=%fused_computation.8.clone.1 | convolution fusion | flops 5470027776 | bytes 136217088 | tf_op jit(solution)/shard_map/while/body/eval_jaxpr/hqk,khe->hqe/dot_general | solution.py:31
  434.4 2.7 copy.11
  437.1 0.7 copy.13
  437.9 0.0 copy-start.3
  437.9 52.5 %fusion.32 = f32[8192,2560]{1,0:T(8,128)} fusion(bf16[320,2560]{1,0:T(8,128)(2,1)S(1)} %copy-done, bf16[8192,2560]{1,0:T(8,128)(2,1)} %all-gather.2.cloned.1.call-done, bf16[2560,320]{0,1:T(8,128)(2,1)} %param.12), kind=kOutput, calls=%fused_computation.28 | convolution fusion | flops 26867138560 | bytes 129105920 | tf_op jit(solution)/shard_map/dot_general | solution.py:50
  490.4 53.2 %convolution_add_fusion = f32[8192,2560]{1,0:T(8,128)} fusion(f32[8192,2560]{1,0:T(8,128)} %fusion.32, bf16[8192,80]{0,1:T(8,128)(2,1)S(1)} %bitcast.56, bf16[1,80,2560]{2,1,0:T(8,128)(2,1)S(1)} %copy-done.3), kind=kOutput, calls=%fused_computation.16 | convolution fusion | flops 3376414720 | bytes 169492480 | tf_op jit(solution)/shard_map/nhqe,hed->nqd/dot_general | solution.py:47
  543.6 0.1 reduce-scatter.2.cloned.1.call-update
  543.7 336.5 %reduce-scatter.2.cloned.1.call-done = f32[256,2560]{1,0:T(8,128)} async-done(((f32[8192,2560]{1,0:T(8,128)}), f32[256,2560]{1,0:T(8,128)}) %reduce-scatter.2.cloned.1.call-update) | async-done | bytes 2621456 | tf_op jit(solution)/shard_map/reduce_scatter | solution.py:51
  880.2 3.1 fusion.43
  (13 shorter events, 0.0 us)
Async XLA Ops:
  6.5 431.3 %copy-start = (bf16[320,2560]{1,0:T(8,128)(2,1)S(1)}, bf16[320,2560]{1,0:T(8,128)(2,1)}, u32[]{:S(2)}) copy-start(bf16[320,2560]{1,0:T(8,128)(2,1)} %param.13) | copy-start | bytes 4915204
  6.6 3.6 copy-start.1
  6.6 3.6 copy-start.4
  6.6 139.9 %all-gather.2.cloned.1.call-start = ((), (), s32[]{:S(2)}) async-start(), calls=%async_computation.1 | async-start | bytes 43253760 | tf_op jit(solution)/shard_map/all_gather | solution.py:43
  11.7 868.5 %reduce-scatter.2.cloned.1.call-start = ((), (), s32[]{:S(2)}) async-start(), calls=%async_computation.2 | async-start | bytes 86507520 | tf_op jit(solution)/shard_map/reduce_scatter | solution.py:51
  437.9 52.5 %copy-start.3 = (bf16[1,80,2560]{2,1,0:T(8,128)(2,1)S(1)}, bf16[1,80,2560]{2,1,0:T(8,128)(2,1)}, u32[]{:S(2)}) copy-start(bf16[1,80,2560]{2,1,0:T(8,128)(2,1)} %param.11) | copy-start | bytes 1228804
  543.6 336.6 %copy-start.2 = (bf16[256,2560]{1,0:T(8,128)(2,1)S(1)}, bf16[256,2560]{1,0:T(8,128)(2,1)}, u32[]{:S(2)}) copy-start(bf16[256,2560]{1,0:T(8,128)(2,1)} %param.8) | copy-start | bytes 3932164
Sparse Core Ops, SparseCore 0:
  11.8 134.6 all-gather.1
  543.8 336.3 reduce-scatter.1
where the time goes:
time: 891 us; the launch traced here: 890 us
  waiting for transfers between devices  471 us (53%)
  matrix products  307 us (34%)
  other arithmetic  90.2 us (10%)
  between operations  13.5 us (2%)
    reduce_scatter x1, waiting for transfers between devices, local_block(): reduced = lax.psum_scatter(part_sum, 'tp', scatter_dimension=0, tiled=True)  337 us
    all_gather x1, waiting for transfers between devices, local_block(): gathered = lax.all_gather(normed, 'tp', axis=0, tiled=True)  135 us
    dot_general x2, matrix products, one_block(): jnp.einsum('qhe,khe->hqk', query_blk, key_rows, preferred_element_type=jn...  92.2 us
    dot_general x2, matrix products, one_block(): jnp.einsum('hqk,khe->hqe', exp_scores.astype(jnp.bfloat16), value_rows, p...  88.7 us
    reduce_sum x2, other arithmetic, one_block(): exp_sum = jnp.sum(exp_scores, axis=-1, keepdims=True)  82.1 us
    dot_general x1, matrix products, local_block(): jnp.einsum('nhqe,hed->nqd', head_out, w_out, preferred_element_type=jnp.f...  53.2 us
    dot_general x1, matrix products, local_block(): jnp.dot(hidden, w_down, preferred_element_type=jnp.float32)  52.5 us
    dot_general x1, matrix products, local_block(): jnp.einsum('sd,dhc->shc', gathered, w_qkv, preferred_element_type=jnp.flo...  20.2 us
  transfers between devices with their start and end apart: 2, of which 2 were waited for; matrix products, arithmetic and copies ran while one was open for 0% of the time, Pallas kernels for 0%

commit v1 on v0

v1 whole, which is shorter than its diff:
```python
import functools
import math
import jax
import jax.numpy as jnp
from jax import lax
from jax.experimental import pallas as pl
from jax.experimental.pallas import tpu as pltpu
from jax.sharding import Mesh, PartitionSpec as P

LN_EPS = 1e-6
BF = jnp.bfloat16
F32 = jnp.float32

def split3(x):
    hi = x.astype(BF)
    r = x - hi.astype(F32)
    mid = r.astype(BF)
    lo = (r - mid.astype(F32)).astype(BF)
    return hi, mid, lo

TK = 256

def attn_kernel(hd, bq, qkv_ref, o_ref, kaug_ref, qaug_ref, sums_ref, acc_ref):
    groups, _, toks = qkv_ref.shape
    keys = groups * toks
    i = pl.program_id(0)
    per = toks // bq
    scale = hd ** -0.5 * math.log2(math.e)
    depth = kaug_ref.shape[1]
    pad = depth - 3 * hd

    @pl.when(i == 0)
    def _():
        ones = jnp.where(lax.broadcasted_iota(jnp.int32, (pad, TK), 0) < 3, 1.0, 0.0).astype(BF)
        for g in range(groups):
            for t in range(toks // TK):
                kt = qkv_ref[g, hd:2 * hd, t * TK:(t + 1) * TK]
                aug = jnp.concatenate([kt, kt, kt, ones], axis=0)
                kaug_ref[pl.ds(g * toks + t * TK, TK), :] = aug.T

    qt = qkv_ref[i // per, 0:hd, pl.ds(pl.multiple_of((i % per) * bq, bq), bq)]
    hi, mid, lo = split3(qt.astype(F32) * scale)
    qaug_ref[0:hd, :] = hi
    qaug_ref[hd:2 * hd, :] = mid
    qaug_ref[2 * hd:3 * hd, :] = lo
    qaug_ref[3 * hd:, :] = jnp.zeros((pad, bq), BF)

    def set_shift(c):
        chi, cmid, clo = split3(-c)
        row = lax.broadcasted_iota(jnp.int32, (pad, bq), 0)
        z = jnp.where(row == 0, chi.astype(F32), jnp.where(row == 1, cmid.astype(F32), jnp.where(row == 2, clo.astype(F32), 0.0)))
        qaug_ref[3 * hd:, :] = z.astype(BF)

    def scores(t):
        return jnp.dot(kaug_ref[pl.ds(t * TK, TK), :], qaug_ref[...], preferred_element_type=F32)

    def main():
        l8 = jnp.zeros((8, bq), F32)
        acc = None
        U = 4
        for u in range(keys // (TK * U)):
            ps = []
            for j in range(U):
                t = u * U + j
                p = jnp.exp2(scores(t))
                l8 = l8 + p.reshape(TK // 8, 8, bq).sum(axis=0)
                ps.append(p.astype(BF))
            k0 = u * U * TK
            vt = qkv_ref[k0 // toks, 2 * hd:3 * hd, k0 % toks:k0 % toks + U * TK]
            d = jnp.dot(vt, jnp.concatenate(ps, axis=0), preferred_element_type=F32)
            acc = d if acc is None else acc + d
        sums_ref[...] = l8
        acc_ref[...] = acc

    set_shift(jnp.max(scores(0), axis=0, keepdims=True))
    main()
    l = jnp.sum(sums_ref[...], axis=0, keepdims=True)
    ok = jnp.logical_and(jnp.max(l) < 2.0 ** 64, jnp.max(jnp.abs(acc_ref[...])) < 3e38)

    @pl.when(jnp.logical_not(ok))
    def _():
        qaug_ref[3 * hd:, :] = jnp.zeros((pad, bq), BF)
        def step(t, m):
            return jnp.maximum(m, jnp.max(scores(t), axis=0, keepdims=True))
        m = lax.fori_loop(0, keys // TK, step, jnp.full((1, bq), -jnp.inf, F32))
        set_shift(m)
        sums_ref[...] = jnp.zeros_like(sums_ref)
        acc_ref[...] = jnp.zeros_like(acc_ref)
        def again(t, c):
            p = jnp.exp2(scores(t))
            sums_ref[...] += p.reshape(TK // 8, 8, bq).sum(axis=0)
            vt = qkv_ref[t // (toks // TK), 2 * hd:3 * hd, pl.ds(pl.multiple_of((t % (toks // TK)) * TK, TK), TK)]
            acc_ref[...] += jnp.dot(vt, p.astype(BF), preferred_element_type=F32)
            return c
        lax.fori_loop(0, keys // TK, again, 0)

    o_ref[0] = (acc_ref[...] / jnp.sum(sums_ref[...], axis=0, keepdims=True)).astype(BF)

def attention(qkv, bq=512):
    groups, three, toks = qkv.shape
    hd = three // 3
    keys = groups * toks
    per = toks // bq
    return pl.pallas_call(
        functools.partial(attn_kernel, hd, bq),
        grid=(groups * per,),
        in_specs=[pl.BlockSpec((groups, three, toks), lambda i: (0, 0, 0))],
        out_specs=pl.BlockSpec((1, hd, bq), lambda i: (i // per, 0, i % per)),
        out_shape=jax.ShapeDtypeStruct((groups, hd, toks), BF),
        scratch_shapes=[pltpu.VMEM((keys, 256), BF), pltpu.VMEM((256, bq), BF), pltpu.VMEM((8, bq), F32), pltpu.VMEM((hd, bq), F32)],
        cost_estimate=pl.CostEstimate(flops=4 * keys * keys * hd, bytes_accessed=2 * keys * 4 * hd, transcendentals=keys * keys),
        name="attention",
    )(qkv)


def layer_norm(row_vals, ln_gain):
    row_mean = jnp.mean(row_vals, axis=-1, keepdims=True)
    centered = row_vals - row_mean
    row_var = jnp.mean(centered * centered, axis=-1, keepdims=True)
    return (centered * lax.rsqrt(row_var + LN_EPS) * ln_gain).astype(BF)


def solution(mesh):
    data, tp = mesh.devices.shape
    side = math.isqrt(tp // 2)
    grid = Mesh(mesh.devices.reshape(data, side, side, tp // (side * side)), ("data", "y", "x", "core"))
    col = ("y", "core")

    def local_block(x_loc, ln_gamma, w_qkv, w_out, w_up, w_down):
        residual = x_loc.astype(F32)
        normed = layer_norm(residual, ln_gamma)
        rows = lax.all_gather(normed, "x", axis=0, tiled=True)
        wqkv = lax.all_gather(w_qkv[:, 0, :], col, axis=0)
        wup = lax.all_gather(w_up, col, axis=0)
        wdown = lax.all_gather(w_down, col, axis=0, tiled=True)
        wout = lax.all_gather(w_out[0], col, axis=0, tiled=True)
        qkv = jnp.einsum("hdc,td->hct", wqkv, rows, preferred_element_type=F32).astype(BF)
        qkv = lax.all_to_all(qkv, col, split_axis=0, concat_axis=0, tiled=True)
        out = attention(qkv)
        out = lax.all_to_all(out, col, split_axis=0, concat_axis=0, tiled=True)
        pre = jnp.einsum("td,hdf->thf", rows, wup, preferred_element_type=F32)
        hidden = jax.nn.gelu(pre, approximate=True).astype(BF)
        part = jnp.dot(hidden.reshape(rows.shape[0], -1), wdown, preferred_element_type=F32)
        part = part + jnp.einsum("et,ed->td", out.reshape(-1, out.shape[2]), wout, preferred_element_type=F32)
        reduced = lax.psum_scatter(part, "x", scatter_dimension=0, tiled=True)
        return (residual + reduced).astype(BF)

    row_spec = P(("data", "y", "x", "core"), None)
    tp_axes = ("y", "x", "core")
    return jax.shard_map(
        local_block,
        mesh=grid,
        in_specs=(row_spec, P(None), P(None, tp_axes, None), P(tp_axes, None, None), P(None, tp_axes), P(tp_axes, None)),
        out_specs=row_spec,
        check_vma=False,
    )
```

time: 891 us -> 476 us (0.53)
  waiting for transfers between devices: 471 us -> 213 us
  matrix products: 307 us -> 67.9 us
  other arithmetic: 90.2 us -> 9.94 us
  Pallas kernels: 0 us -> 73.5 us
  blocking collectives: 0 us -> 71 us
  local copies, waits for them, and re-layouts: 8.14 us -> 22.2 us
    dot_general x7 -> x3, matrix products: 307 us -> 53.4 us  [the longest x1 22.8 us: local_block(): jnp.dot(hidden.reshape(rows.shape[0], -1), wdown, preferred_element_type=...]
    reduce_scatter x1, waiting for transfers between devices: 337 us -> 94.5 us  [local_block(): reduced = lax.psum_scatter(part, 'x', scatter_dimension=0, tiled=True)]
    reduce_sum x2 -> x0, other arithmetic: 82.1 us -> none  [one_block(): exp_sum = jnp.sum(exp_scores, axis=-1, keepdims=True)]
    pallas_call x0 -> x1, Pallas kernels: none -> 73.5 us  [attention(): pl.pallas_call(functools.partial(attn_kernel, hd, bq), grid=(groups * per...]
    all_to_all x0 -> x1, blocking collectives: none -> 71 us  [local_block(): qkv = lax.all_to_all(qkv, col, split_axis=0, concat_axis=0, tiled=True)]
    all_gather x1 -> x5, waiting for transfers between devices: 135 us -> 84 us  [the longest x1 50.7 us: local_block(): wqkv = lax.all_gather(w_qkv[:, 0, :], col, axis=0)]
    all_to_all x0 -> x1, waiting for transfers between devices: none -> 32.1 us  [local_block(): out = lax.all_to_all(out, col, split_axis=0, concat_axis=0, tiled=True)]
    unnamed x0 -> x1, matrix products: none -> 14.5 us
  transfers between devices with their start and end apart: 2 -> 7, of which waited for: 2 -> 4; matrix products, arithmetic and copies ran while one was open for 0% -> 16% of each run, Pallas kernels for 0% -> 15%
where the time goes in v1:
time: 476 us
  waiting for transfers between devices  213 us (45%)
  Pallas kernels  73.5 us (15%)
  blocking collectives  71 us (15%)
  matrix products  67.9 us (14%)
  local copies, waits for them, and re-layouts  22.2 us (5%)
  between operations  13.5 us (3%)
  other arithmetic  9.94 us (2%)
    reduce_scatter x1, waiting for transfers between devices, local_block(): reduced = lax.psum_scatter(part, 'x', scatter_dimension=0, tiled=True)  94.5 us
    pallas_call x1, Pallas kernels, attention(): pl.pallas_call(functools.partial(attn_kernel, hd, bq), grid=(groups * per...  73.5 us
    all_to_all x1, blocking collectives, local_block(): qkv = lax.all_to_all(qkv, col, split_axis=0, concat_axis=0, tiled=True)  71 us
    all_gather x1, waiting for transfers between devices, local_block(): wqkv = lax.all_gather(w_qkv[:, 0, :], col, axis=0)  50.7 us
    all_gather x1, waiting for transfers between devices, local_block(): rows = lax.all_gather(normed, 'x', axis=0, tiled=True)  33.3 us
    all_to_all x1, waiting for transfers between devices, local_block(): out = lax.all_to_all(out, col, split_axis=0, concat_axis=0, tiled=True)  32.1 us
    dot_general x1, matrix products, local_block(): jnp.dot(hidden.reshape(rows.shape[0], -1), wdown, preferred_element_type=...  22.8 us
    dot_general x1, matrix products, local_block(): pre = jnp.einsum('td,hdf->thf', rows, wup, preferred_element_type=F32)  21.9 us
  transfers between devices with their start and end apart: 7, of which 4 were waited for; matrix products, arithmetic and copies ran while one was open for 16% of the time, Pallas kernels for 15%

profile of v1, /device:TPU:97, one launch (start us, length us, event | category | flops | bytes accessed | tf_op | source)
XLA Modules:
  0.0 475.9 jit_solution(10998066091863365882)
XLA Ops:
  6.6 0.7 all-gather.15.cloned.1.call-update
  7.4 1.6 convert_reduce_fusion
  9.0 1.8 fusion.18
  10.8 2.8 fusion.20
  13.7 0.1 all-gather.17.cloned.1.call-start
  13.7 0.7 all-gather.17.cloned.1.call-update
  14.5 0.6 all-gather.13.cloned.1.call-update
  15.1 0.1 all-gather.11.cloned.1.call-start
  15.2 0.6 all-gather.11.cloned.1.call-update
  15.8 50.7 %all-gather.15.cloned.1.call-done = bf16[20480,1,240]{0,2,1:T(8,128)(2,1)} async-done(((bf16[2560,1,240]{0,2,1:T(8,128)(2,1)}), bf16[20480,1,240]{0,2,1:T(8,128)(2,1)}) %all-gather.15.cloned.1.call-update) | async-done | bytes 9830416 | tf_op jit(solution)/shard_map/all_gather | solution.py:133
  66.4 11.5 %copy.10 = bf16[30,8,8,2560]{3,2,1,0:T(8,128)(2,1)} copy(bf16[30,8,8,2560]{3,1,2,0:T(8,128)(2,1)} %bitcast.31) | data formatting | bytes 19660800
  78.0 10.6 %copy.8 = bf16[8,2560,240]{1,2,0:T(8,128)(2,1)} copy(bf16[8,2560,240]{1,0,2:T(8,128)(2,1)} %bitcast.30) | data formatting | bytes 19660800 | tf_op jit(solution)/shard_map/all_gather | solution.py:133
  88.6 33.3 %all-gather.9.cloned.1.call-done = bf16[1024,2560]{1,0:T(8,128)(2,1)} async-done(((bf16[256,2560]{1,0:T(8,128)(2,1)}), bf16[1024,2560]{1,0:T(8,128)(2,1)}) %all-gather.9.cloned.1.call-update) | async-done | bytes 5242896 | tf_op jit(solution)/shard_map/all_gather | solution.py:132
  121.9 14.5 %fusion.22 = f32[1024,1920]{0,1:S(1)} fusion(bf16[1024,2560]{1,0:T(8,128)(2,1)} %all-gather.9.cloned.1.call-done, bf16[2560,1920]{0,1:T(8,128)(2,1)} %bitcast.32), kind=kOutput, calls=%fused_computation.28 | convolution fusion | flops 10066329600 | bytes 22937600
  136.5 0.6 convert_bitcast_fusion
  137.1 71.0 %all_to_all.10.qkv_ref = bf16[8,240,1024]{2,1,0:T(8,128)(2,1)} all-to-all(bf16[8,240,1024]{2,1,0:T(8,128)(2,1)S(1)} %convert_bitcast_fusion), channel_id=1, replica_groups=mesh['data'=1,'y'=4,'x'=4,'core'=2] {'y','core'}, dimensions={0} | all-to-all | bytes 7864320 | tf_op jit(solution)/shard_map/all_to_all | solution.py:138
  208.1 73.5 %attention.1 = bf16[8,80,1024]{2,1,0:T(8,128)(2,1)} custom-call(bf16[8,240,1024]{2,1,0:T(8,128)(2,1)} %all_to_all.10.qkv_ref), custom_call_target="tpu_custom_call" | custom-call | flops 21474836480 | bytes 5242880 | tf_op jit(solution)/shard_map/attention/pallas_call | solution.py:104
  281.6 4.3 all-to-all-start.1
  285.9 32.1 %all-to-all-done.1 = bf16[8,80,1024]{2,1,0:T(8,128)(2,1)S(1)} async-done(((bf16[8,80,1024]{2,1,0:T(8,128)(2,1)}), bf16[8,80,1024]{2,1,0:T(8,128)(2,1)S(1)}, u32[]{:S(2)}, u32[]{:S(2)}) %all-to-all-start.1) | async-done | bytes 1310752 | tf_op jit(solution)/shard_map/all_to_all | solution.py:140
  318.0 8.7 %fusion.14 = f32[1024,2560]{1,0:T(8,128)} fusion(bf16[640,1024]{1,0:T(8,128)(2,1)S(1)} %bitcast.34, bf16[1,640,2560]{2,1,0:T(8,128)(2,1)} %all-gather.17.cloned.1.call-done), kind=kOutput, calls=%fused_computation.18 | convolution fusion | flops 3355443200 | bytes 15073280 | tf_op jit(solution)/shard_map/et,ed->td/dot_general | solution.py:144
  326.7 21.9 %fusion.10 = bf16[1024,8,320]{0,2,1:T(8,128)(2,1)} fusion(bf16[40,8,8,2560]{3,2,1,0:T(8,128)(2,1)} %bitcast.35, bf16[1024,2560]{1,0:T(8,128)(2,1)} %all-gather.9.cloned.1.call-done), kind=kOutput, calls=%fused_computation.11 | convolution fusion | flops 13445365760 | bytes 23592960 | tf_op jit(solution)/shard_map/td,hdf->thf/dot_general | solution.py:141
  348.6 22.8 %convolution_add_fusion = f32[1024,2560]{1,0:T(8,128)} fusion(f32[1024,2560]{1,0:T(8,128)} %fusion.14, bf16[1024,2560]{0,1:T(8,128)(2,1)} %bitcast.36, bf16[2560,2560]{1,0:T(8,128)(2,1)} %all-gather.11.cloned.1.call-done), kind=kOutput, calls=%fused_computation.12 | convolution fusion | flops 13424394240 | bytes 39321600 | tf_op jit(solution)/shard_map/dot_general | solution.py:143
  371.4 94.5 %reduce-scatter.2.cloned.1.call-done = f32[256,2560]{1,0:T(8,128)} async-done(((f32[1024,2560]{1,0:T(8,128)}), f32[256,2560]{1,0:T(8,128)}) %reduce-scatter.2.cloned.1.call-update) | async-done | bytes 2621456 | tf_op jit(solution)/shard_map/reduce_scatter | solution.py:145
  465.9 3.1 fusion.21
  (13 shorter events, 0.3 us)
Async XLA Ops:
  6.5 59.9 %all-gather.15.cloned.1.call-start = ((), (), s32[]{:S(2)}) async-start(), calls=%async_computation.7 | async-start | bytes 11059200 | tf_op jit(solution)/shard_map/all_gather | solution.py:133
  7.3 114.6 %all-gather.9.cloned.1.call-start = ((), (), s32[]{:S(2)}) async-start(), calls=%async_computation.3 | async-start | bytes 6553600 | tf_op jit(solution)/shard_map/all_gather | solution.py:132
  13.7 272.2 %all-gather.17.cloned.1.call-start = ((), (), s32[]{:S(2)}) async-start(), calls=%async_computation.8 | async-start | bytes 3686400 | tf_op jit(solution)/shard_map/all_gather | solution.py:136
  14.5 312.2 %all-gather.13.cloned.1.call-start = ((), (), s32[]{:S(2)}) async-start(), calls=%async_computation.6 | async-start | bytes 14745600 | tf_op jit(solution)/shard_map/all_gather | solution.py:134
  15.1 333.5 %all-gather.11.cloned.1.call-start = ((), (), s32[]{:S(2)}) async-start(), calls=%async_computation.4 | async-start | bytes 14745600 | tf_op jit(solution)/shard_map/all_gather | solution.py:135
  281.6 36.4 %all-to-all-start.1 = ((bf16[8,80,1024]{2,1,0:T(8,128)(2,1)}), bf16[8,80,1024]{2,1,0:T(8,128)(2,1)S(1)}, u32[]{:S(2)}, u32[]{:S(2)}) async-start(bf16[8,80,1024]{2,1,0:T(8,128)(2,1)} %attention.1), calls=%async_computation.1 | async-start | bytes 2621440 | tf_op jit(solution)/shard_map/all_to_all | solution.py:140
  285.9 180.0 %reduce-scatter.2.cloned.1.call-start = ((), (), s32[]{:S(2)}) async-start(), calls=%async_computation.5 | async-start | bytes 13107200 | tf_op jit(solution)/shard_map/reduce_scatter | solution.py:145
  371.4 94.6 %copy-start = (bf16[256,2560]{1,0:T(8,128)(2,1)S(1)}, bf16[256,2560]{1,0:T(8,128)(2,1)}, u32[]{:S(2)}) copy-start(bf16[256,2560]{1,0:T(8,128)(2,1)} %param.6) | copy-start | bytes 3932164
Sparse Core Ops, SparseCore 0:
  8.9 57.4 all-gather.14
  68.0 53.8 all-gather.8
  123.5 31.4 all-gather.16
  156.5 88.8 all-gather.12
  246.9 80.8 all-gather.10
  371.5 94.3 reduce-scatter.1

commit v2 on v0

v2 whole, which is shorter than its diff:
```python
import functools
import math
import jax
import jax.numpy as jnp
from jax import lax
from jax.experimental import pallas as pl
from jax.experimental.pallas import tpu as pltpu
from jax.sharding import Mesh, PartitionSpec as P

LN_EPS = 1e-6
BF = jnp.bfloat16
F32 = jnp.float32
TK = 256
TRIP = 16
ROWS = 64


def attn_kernel(hd, cores, sub, qkv_ref, o_ref, kaug_ref, qaug_ref, m_ref, sa_ref, sb_ref, acc_ref):
    groups, _, toks = qkv_ref.shape
    keys = groups * toks
    bq = sa_ref.shape[1]
    subs = bq // sub
    i = pl.program_id(0)
    scale = hd ** -0.5 * math.log2(math.e)
    pad = kaug_ref.shape[1] - 3 * hd
    chunk = TRIP * TK

    def load_query(b, slot):
        b = jnp.minimum(b, 2 * pl.num_programs(0) - 1)
        dest, part = b // 2, b % 2
        for j in range(subs):
            g = (part * subs + j) * cores + dest % cores
            at = pl.multiple_of((dest // cores) * sub, sub)
            qt = qkv_ref[g, 0:hd, pl.ds(at, sub)].astype(F32) * scale
            hi = qt.astype(BF)
            rest = qt - hi.astype(F32)
            mid = rest.astype(BF)
            cols = slice(j * sub, (j + 1) * sub)
            qaug_ref[slot, 0:hd, cols] = hi
            qaug_ref[slot, hd:2 * hd, cols] = mid
            qaug_ref[slot, 2 * hd:3 * hd, cols] = (rest - mid.astype(F32)).astype(BF)

    def fold(piece, op):
        return op(piece.reshape(piece.shape[0] // 8, 8, bq), axis=0)

    @pl.when(i == 0)
    def _():
        zeros = jnp.zeros((pad, TK), BF)

        def spread(t, c):
            g = t * TK // toks
            t0 = pl.multiple_of(t * TK - g * toks, TK)
            kt = qkv_ref[g, hd:2 * hd, pl.ds(t0, TK)]
            kaug_ref[pl.ds(pl.multiple_of(t * TK, TK), TK), :] = jnp.concatenate([kt, kt, kt, zeros], axis=0).T
            return c

        lax.fori_loop(0, keys // TK, spread, 0, unroll=4)
        qaug_ref[:, 3 * hd:, :] = jnp.zeros((2, pad, bq), BF)
        load_query(0, 0)
        load_query(1, 1)

        def first(c, m8):
            at = pl.ds(pl.multiple_of(c * 4 * TK, 4 * TK), 4 * TK)
            s = jnp.dot(kaug_ref[at, :], qaug_ref[0], preferred_element_type=F32)
            sa_ref[at, :] = s
            return jnp.maximum(m8, fold(s, jnp.max))

        m8 = lax.fori_loop(0, keys // (4 * TK), first, jnp.full((8, bq), -jnp.inf, F32))
        m_ref[...] = jnp.max(m8, axis=0, keepdims=True)

    def half(s_in, s_out, slot, col):
        m = m_ref[...]
        acc_ref[...] = jnp.zeros_like(acc_ref)

        def trip(c, carry):
            m8, l8 = carry
            k0 = pl.multiple_of(c * chunk, chunk)
            total = None
            for u in range(TRIP):
                s_new = jnp.dot(kaug_ref[pl.ds(k0 + u * TK, TK), :], qaug_ref[slot], preferred_element_type=F32)
                ps = []
                for r in range(0, TK, ROWS):
                    p = jnp.exp2(s_in[pl.ds(k0 + u * TK + r, ROWS), :] - m)
                    l8 = l8 + fold(p, jnp.sum)
                    ps.append(p.astype(BF))
                at = u * TK % toks
                vt = qkv_ref[k0 // toks + u * TK // toks, 2 * hd:3 * hd, at:at + TK]
                d = jnp.dot(vt, jnp.concatenate(ps, axis=0), preferred_element_type=F32)
                total = d if total is None else total + d
                for r in range(0, TK, ROWS):
                    piece = s_new[r:r + ROWS]
                    m8 = jnp.maximum(m8, fold(piece, jnp.max))
                    s_out[pl.ds(k0 + u * TK + r, ROWS), :] = piece
            acc_ref[...] += total
            return m8, l8

        m8, l8 = lax.fori_loop(0, keys // chunk, trip, (jnp.full((8, bq), -jnp.inf, F32), jnp.zeros((8, bq), F32)))
        o_ref[0, :, col:col + bq] = (acc_ref[...] / jnp.sum(l8, axis=0, keepdims=True)).astype(BF)
        m_ref[...] = jnp.max(m8, axis=0, keepdims=True)

    half(sa_ref, sb_ref, 1, 0)
    load_query(2 * i + 2, 0)
    half(sb_ref, sa_ref, 0, bq)
    load_query(2 * i + 3, 1)


def attention(qkv, cores, side):
    groups, three, toks = qkv.shape
    hd = three // 3
    keys = groups * toks
    bq = toks // 2
    return pl.pallas_call(
        functools.partial(attn_kernel, hd, cores, toks // side),
        grid=(groups,),
        in_specs=[pl.BlockSpec((groups, three, toks), lambda i: (0, 0, 0))],
        out_specs=pl.BlockSpec((1, hd, toks), lambda i: (i, 0, 0)),
        out_shape=jax.ShapeDtypeStruct((groups, hd, toks), BF),
        scratch_shapes=[
            pltpu.VMEM((keys, 256), BF),
            pltpu.VMEM((2, 256, bq), BF),
            pltpu.VMEM((1, bq), F32),
            pltpu.VMEM((keys, bq), F32),
            pltpu.VMEM((keys, bq), F32),
            pltpu.VMEM((hd, bq), F32),
        ],
        compiler_params=pltpu.CompilerParams(vmem_limit_bytes=58 * 1024 * 1024),
        cost_estimate=pl.CostEstimate(flops=6 * keys * keys * hd, bytes_accessed=8 * keys * hd, transcendentals=keys * keys),
        name="attention",
    )(qkv)


def layer_norm(row_vals, ln_gain):
    row_mean = jnp.mean(row_vals, axis=-1, keepdims=True)
    centered = row_vals - row_mean
    row_var = jnp.mean(centered * centered, axis=-1, keepdims=True)
    return (centered * lax.rsqrt(row_var + LN_EPS) * ln_gain).astype(BF)


def ring_gather(block, axis, side):
    up = [(j, (j + 1) % side) for j in range(side)]
    down = [(j, (j - 1) % side) for j in range(side)]
    rows = block.shape[0]
    half = rows // 2
    before = lax.ppermute(block, axis, up)
    after = lax.ppermute(block, axis, down)
    far_a = lax.ppermute(before[:half], axis, up)
    far_b = lax.ppermute(after[half:], axis, down)
    me = lax.axis_index(axis)
    full = jnp.zeros((side * rows, block.shape[1]), block.dtype)
    place = lambda full, part, pos, off: lax.dynamic_update_slice(full, part, (pos % side * rows + off, 0))
    full = place(full, block, me, 0)
    full = place(full, before, me - 1 + side, 0)
    full = place(full, after, me + 1, 0)
    full = place(full, far_a, me + 2, 0)
    return place(full, far_b, me + 2, half)


def solution(mesh):
    data, tp = mesh.devices.shape
    side = math.isqrt(tp // 2)
    cores = tp // (side * side)
    grid = Mesh(mesh.devices.reshape(data, side, side, cores), ("data", "y", "x", "core"))
    row, col = ("x", "core"), ("y", "core")

    def local_block(x_loc, ln_gamma, w_qkv, w_out, w_up, w_down):
        residual = x_loc.astype(F32)
        normed = layer_norm(residual, ln_gamma)
        wqkv = lax.all_gather(w_qkv[:, 0, :].T, row, axis=0, tiled=True)
        tall = ring_gather(normed, "y", side)
        qkv = lax.dot_general(wqkv, tall, (((1,), (1,)), ((), ())), preferred_element_type=F32).astype(BF)
        qkv = qkv.reshape(side * cores, -1, tall.shape[0])
        qkv = lax.all_to_all(qkv, row, split_axis=0, concat_axis=0, tiled=True)
        qkv, normed = lax.optimization_barrier((qkv, normed))
        wide = ring_gather(normed, "x", side)
        out = attention(qkv, cores, side)
        out = lax.all_to_all(out, col, split_axis=0, concat_axis=0, tiled=True)
        out = out.reshape(-1, out.shape[2])
        wup = lax.all_gather(w_up.T, col, axis=0, tiled=True)
        wout = lax.all_gather(w_out[0], col, axis=0, tiled=True)
        wdown = lax.all_gather(w_down, col, axis=0, tiled=True)
        pre = lax.dot_general(wide, wup, (((1,), (1,)), ((), ())), preferred_element_type=F32)
        hidden = jax.nn.gelu(pre, approximate=True).astype(BF)
        width = wdown.shape[1]
        cuts = [0, width // 5, 3 * width // 5, width]
        reduced = []
        for a, b in zip(cuts[:-1], cuts[1:]):
            part = jnp.dot(hidden, wdown[:, a:b], preferred_element_type=F32)
            part = part + lax.dot_general(out, wout[:, a:b], (((0,), (0,)), ((), ())), preferred_element_type=F32)
            reduced.append(lax.psum_scatter(part, "x", scatter_dimension=0, tiled=True))
        return (residual + jnp.concatenate(reduced, axis=1)).astype(BF)

    row_spec = P(("data", "y", "x", "core"), None)
    tp_axes = ("y", "x", "core")
    return jax.shard_map(
        local_block,
        mesh=grid,
        in_specs=(row_spec, P(None), P(None, tp_axes, None), P(tp_axes, None, None), P(None, tp_axes), P(tp_axes, None)),
        out_specs=row_spec,
        check_vma=False,
    )
```

time: 891 us -> 427 us (0.48)
  waiting for transfers between devices: 471 us -> 187 us
  matrix products: 307 us -> 77.6 us
  Pallas kernels: 0 us -> 86.4 us
  other arithmetic: 90.2 us -> 5.79 us
  starting transfers between devices: 0.07 us -> 26.6 us
  local copies, waits for them, and re-layouts: 8.14 us -> 29.5 us
    reduce_scatter x1 -> x3, waiting for transfers between devices: 337 us -> 92.8 us  [local_block(): reduced.append(lax.psum_scatter(part, 'x', scatter_dimension=0, tiled=True))]
    dot_general x7 -> x8, matrix products: 307 us -> 77.6 us  [the longest x3 25.6 us: local_block(): part = jnp.dot(hidden, wdown[:, a:b], preferred_element_type=F32)]
    all_gather x1 -> x4, waiting for transfers between devices: 135 us -> 0.01 us  [the longest x1 0.01 us: local_block(): wqkv = lax.all_gather(w_qkv[:, 0, :].T, row, axis=0, tiled=True)]
    pallas_call x0 -> x1, Pallas kernels: none -> 86.4 us  [attention(): pl.pallas_call(functools.partial(attn_kernel, hd, cores, toks // side), g...]
    reduce_sum x2 -> x0, other arithmetic: 82.1 us -> none  [one_block(): exp_sum = jnp.sum(exp_scores, axis=-1, keepdims=True)]
    ppermute x0 -> x8, waiting for transfers between devices: none -> 46 us  [the longest x2 28.7 us: ring_gather(): before = lax.ppermute(block, axis, up)]
    all_to_all x0 -> x2, waiting for transfers between devices: none -> 45.1 us  [the longest x1 45.1 us: local_block(): qkv = lax.all_to_all(qkv, row, split_axis=0, concat_axis=0, tiled=True)]
    dynamic_update_slice x0 -> x9, local copies, waits for them, and re-layouts: none -> 14.6 us  [ring_gather(): lax.dynamic_update_slice(full, part, (pos % side * rows + off, 0))]
  transfers between devices with their start and end apart: 2 -> 17, of which waited for: 2 -> 7; matrix products, arithmetic and copies ran while one was open for 0% -> 25% of each run, Pallas kernels for 0% -> 20%
where the time goes in v2:
time: 427 us; the launch traced here: 426 us
  waiting for transfers between devices  187 us (44%)
  Pallas kernels  86.4 us (20%)
  matrix products  77.6 us (18%)
  local copies, waits for them, and re-layouts  29.5 us (7%)
  starting transfers between devices  26.6 us (6%)
  between operations  13.7 us (3%)
  other arithmetic  5.79 us (1%)
    reduce_scatter x3, waiting for transfers between devices, local_block(): reduced.append(lax.psum_scatter(part, 'x', scatter_dimension=0, tiled=True))  92.8 us
    pallas_call x1, Pallas kernels, attention(): pl.pallas_call(functools.partial(attn_kernel, hd, cores, toks // side), g...  86.4 us
    all_to_all x1, waiting for transfers between devices, local_block(): qkv = lax.all_to_all(qkv, row, split_axis=0, concat_axis=0, tiled=True)  45.1 us
    ppermute x2, waiting for transfers between devices, ring_gather(): before = lax.ppermute(block, axis, up)  28.7 us
    dot_general x3, matrix products, local_block(): part = jnp.dot(hidden, wdown[:, a:b], preferred_element_type=F32)  25.6 us
    dot_general x1, matrix products, local_block(): lax.dot_general(wide, wup, (((1,), (1,)), ((), ())), preferred_element_ty...  21.1 us
    ppermute x2, waiting for transfers between devices, ring_gather(): far_a = lax.ppermute(before[:half], axis, up)  17.3 us
    dot_general x1, matrix products, local_block(): lax.dot_general(wqkv, tall, (((1,), (1,)), ((), ())), preferred_element_t...  16.6 us
  transfers between devices with their start and end apart: 17, of which 7 were waited for; matrix products, arithmetic and copies ran while one was open for 25% of the time, Pallas kernels for 20%

profile of v2, /device:TPU:97, one launch (start us, length us, event | category | flops | bytes accessed | tf_op | source)
XLA Modules:
  0.0 426.5 jit_solution(11861302042114742639)
XLA Ops:
  9.7 2.6 broadcast.32.clone
  14.3 2.6 collective-permute-start
  19.5 28.6 %collective-permute-done = bf16[256,2560]{1,0:T(8,128)(2,1)S(1)} collective-permute-done((bf16[256,2560]{1,0:T(8,128)(2,1)}, bf16[256,2560]{1,0:T(8,128)(2,1)S(1)}, u32[]{:S(2)}, u32[]{:S(2)}) %collective-permute-start) | collective-permute-done | bytes 1310752 | tf_op jit(solution)/shard_map/ppermute | solution.py:144
  49.4 2.7 collective-permute-start.3
  55.8 8.9 %collective-permute-done.2 = bf16[128,2560]{1,0:T(8,128)(2,1)S(1)} collective-permute-done((bf16[128,2560]{1,0:T(8,128)(2,1)S(1)}, bf16[128,2560]{1,0:T(8,128)(2,1)S(1)}, u32[]{:S(2)}, u32[]{:S(2)}) %collective-permute-start.2) | collective-permute-done | bytes 655392 | tf_op jit(solution)/shard_map/ppermute | solution.py:146
  66.4 16.6 %convert_bitcast_fusion = bf16[1920,1024]{0,1:T(8,128)(2,1)} fusion(bf16[1024,2560]{1,0:T(8,128)(2,1)} %constant_dynamic-update-slice_fusion.5, bf16[1920,2560]{1,0:T(8,128)(2,1)} %all-gather.6.cloned.1.call-done), kind=kOutput, calls=%fused_computation.13 | convolution fusion | flops 10068295680 | bytes 19005440 | tf_op jit(solution)/shard_map/dot_general | solution.py:170
  83.0 6.3 %copy.7 = bf16[1920,1024]{1,0:T(8,128)(2,1)} copy(bf16[1920,1024]{0,1:T(8,128)(2,1)} %convert_bitcast_fusion) | data formatting | bytes 7864320 | tf_op jit(solution)/shard_map/convert_element_type | solution.py:170
  89.3 6.4 %all-to-all-start = ((bf16[8,240,1024]{2,1,0:T(8,128)(2,1)}), bf16[8,240,1024]{2,1,0:T(8,128)(2,1)}, u32[]{:S(2)}, u32[]{:S(2)}) async-start(bf16[8,240,1024]{2,1,0:T(8,128)(2,1)} %bitcast.22), calls=%async_computation | async-start | bytes 7864320 | tf_op jit(solution)/shard_map/all_to_all | solution.py:172
  96.4 45.1 %all-to-all-done.qkv_ref = bf16[8,240,1024]{2,1,0:T(8,128)(2,1)} async-done(((bf16[8,240,1024]{2,1,0:T(8,128)(2,1)}), bf16[8,240,1024]{2,1,0:T(8,128)(2,1)}, u32[]{:S(2)}, u32[]{:S(2)}) %all-to-all-start) | async-done | bytes 3932192 | tf_op jit(solution)/shard_map/all_to_all | solution.py:172
  144.2 86.4 %attention.1 = bf16[8,80,1024]{2,1,0:T(8,128)(2,1)} custom-call(bf16[8,240,1024]{2,1,0:T(8,128)(2,1)} %all-to-all-done.qkv_ref), custom_call_target="tpu_custom_call" | custom-call | flops 32212254720 | bytes 5242880 | tf_op jit(solution)/shard_map/attention/pallas_call | solution.py:112
  230.5 6.2 %all-to-all-start.1 = ((bf16[8,80,1024]{2,1,0:T(8,128)(2,1)}), bf16[8,80,1024]{2,1,0:T(8,128)(2,1)S(1)}, u32[]{:S(2)}, u32[]{:S(2)}) async-start(bf16[8,80,1024]{2,1,0:T(8,128)(2,1)} %attention.1), calls=%async_computation.1 | async-start | bytes 2621440 | tf_op jit(solution)/shard_map/all_to_all | solution.py:176
  236.8 2.6 broadcast.32
  244.3 2.7 collective-permute-start.7
  252.0 8.4 %collective-permute-done.6 = bf16[128,2560]{1,0:T(8,128)(2,1)S(1)} collective-permute-done((bf16[128,2560]{1,0:T(8,128)(2,1)S(1)}, bf16[128,2560]{1,0:T(8,128)(2,1)S(1)}, u32[]{:S(2)}, u32[]{:S(2)}) %collective-permute-start.6) | collective-permute-done | bytes 655392 | tf_op jit(solution)/shard_map/ppermute | solution.py:146
  262.2 21.1 %fusion.7 = bf16[1024,2560]{1,0:T(8,128)(2,1)} fusion(bf16[1024,2560]{1,0:T(8,128)(2,1)} %constant_dynamic-update-slice_fusion, bf16[2560,2560]{1,0:T(8,128)(2,1)} %all-gather.8.cloned.1.call-done), kind=kOutput, calls=%fused_computation.8 | convolution fusion | flops 13445365760 | bytes 23592960 | tf_op jit(solution)/shard_map/dot_general | solution.py:181
  283.3 7.5 %fusion.18 = f32[1024,512]{1,0:T(8,128)} fusion(bf16[1024,2560]{1,0:T(8,128)(2,1)} %fusion.7, bf16[2560,2560]{1,0:T(8,128)(2,1)} %all-gather.10.cloned.1.call-done), kind=kOutput, calls=%fused_computation.23 | convolution fusion | flops 2684354560 | bytes 9961472 | tf_op jit(solution)/shard_map/dot_general | solution.py:187
  290.8 4.1 convolution_add_fusion.2
  295.0 9.1 %fusion.10 = f32[1024,1024]{1,0:T(8,128)S(1)} fusion(bf16[1024,2560]{1,0:T(8,128)(2,1)} %fusion.7, bf16[2560,2560]{1,0:T(8,128)(2,1)} %all-gather.10.cloned.1.call-done), kind=kOutput, calls=%fused_computation.11 | convolution fusion | flops 5368709120 | bytes 14680064 | tf_op jit(solution)/shard_map/dot_general | solution.py:187
  304.1 5.1 %convolution_add_fusion.1 = f32[1024,1024]{1,0:T(8,128)} fusion(f32[1024,1024]{1,0:T(8,128)S(1)} %fusion.10, bf16[640,1024]{1,0:T(8,128)(2,1)S(1)} %bitcast.20, bf16[640,2560]{1,0:T(8,128)(2,1)} %bitcast.24), kind=kOutput, calls=%fused_computation.26 | convolution fusion | flops 1343225856 | bytes 11010048 | tf_op jit(solution)/shard_map/dot_general | solution.py:188
  309.6 9.1 %fusion.8 = f32[1024,1024]{1,0:T(8,128)S(1)} fusion(bf16[1024,2560]{1,0:T(8,128)(2,1)} %fusion.7, bf16[2560,2560]{1,0:T(8,128)(2,1)} %all-gather.10.cloned.1.call-done), kind=kOutput, calls=%fused_computation.9 | convolution fusion | flops 5368709120 | bytes 14680064 | tf_op jit(solution)/shard_map/dot_general | solution.py:187
  318.7 5.1 %convolution_add_fusion = f32[1024,1024]{1,0:T(8,128)} fusion(f32[1024,1024]{1,0:T(8,128)S(1)} %fusion.8, bf16[640,1024]{1,0:T(8,128)(2,1)S(1)} %bitcast.21, bf16[640,2560]{1,0:T(8,128)(2,1)} %bitcast.25), kind=kOutput, calls=%fused_computation.25 | convolution fusion | flops 1343225856 | bytes 11010048 | tf_op jit(solution)/shard_map/dot_general | solution.py:188
  324.1 46.2 %reduce-scatter.6.cloned.1.call-done = f32[256,1024]{1,0:T(8,128)} async-done(((f32[1024,1024]{1,0:T(8,128)}), f32[256,1024]{1,0:T(8,128)}) %reduce-scatter.6.cloned.1.call-update) | async-done | bytes 1048592 | tf_op jit(solution)/shard_map/reduce_scatter | solution.py:189
  370.2 46.3 %reduce-scatter.8.cloned.1.call-done = f32[256,1024]{1,0:T(8,128)} async-done(((f32[1024,1024]{1,0:T(8,128)}), f32[256,1024]{1,0:T(8,128)}) %reduce-scatter.8.cloned.1.call-update) | async-done | bytes 1048592 | tf_op jit(solution)/shard_map/reduce_scatter | solution.py:189
  416.6 3.0 fusion.17
  (52 shorter events, 29.9 us)
Async XLA Ops:
  6.5 2.4 copy-start
  6.5 59.9 %all-gather.6.cloned.1.call-start = ((), (), s32[]{:S(2)}) async-start(), calls=%async_computation.5 | async-start | bytes 11059200 | tf_op jit(solution)/shard_map/all_gather | solution.py:168
  7.3 254.9 %all-gather.8.cloned.1.call-start = ((), (), s32[]{:S(2)}) async-start(), calls=%async_computation.6 | async-start | bytes 14745600 | tf_op jit(solution)/shard_map/all_gather | solution.py:178
  8.1 275.2 %all-gather.10.cloned.1.call-start = ((), (), s32[]{:S(2)}) async-start(), calls=%async_computation.7 | async-start | bytes 14745600 | tf_op jit(solution)/shard_map/all_gather | solution.py:180
  8.9 3.4 copy-start.1
  14.3 33.8 %collective-permute-start = (bf16[256,2560]{1,0:T(8,128)(2,1)}, bf16[256,2560]{1,0:T(8,128)(2,1)S(1)}, u32[]{:S(2)}, u32[]{:S(2)}) collective-permute-start(bf16[256,2560]{1,0:T(8,128)(2,1)} %get-tuple-element.7), channel_id=1, source_target_pairs={{0,8},{8,16},{16,24},{24,0},{1,9},{9,17},{17,25},{25,1},{2,10},{10... | collective-permute-start | bytes 3932168 | tf_op jit(solution)/shard_map/ppermute | solution.py:144
  17.0 31.3 %collective-permute-start.1 = (bf16[256,2560]{1,0:T(8,128)(2,1)}, bf16[256,2560]{1,0:T(8,128)(2,1)}, u32[]{:S(2)}, u32[]{:S(2)}) collective-permute-start(bf16[256,2560]{1,0:T(8,128)(2,1)} %get-tuple-element.7), channel_id=1, source_target_pairs={{0,24},{8,0},{16,8},{24,16},{1,25},{9,1},{17,9},{25,17},{2,26},{10... | collective-permute-start | bytes 3932168 | tf_op jit(solution)/shard_map/ppermute | solution.py:145
  48.2 16.5 %collective-permute-start.2 = (bf16[128,2560]{1,0:T(8,128)(2,1)S(1)}, bf16[128,2560]{1,0:T(8,128)(2,1)S(1)}, u32[]{:S(2)}, u32[]{:S(2)}) collective-permute-start(bf16[128,2560]{1,0:T(8,128)(2,1)S(1)} %slice.40), channel_id=1, source_target_pairs={{0,8},{8,16},{16,24},{24,0},{1,9},{9,17},{17,25},{25,1},{2,10},{10... | collective-permute-start | bytes 1966088 | tf_op jit(solution)/shard_map/ppermute | solution.py:146
  49.4 16.1 %collective-permute-start.3 = (bf16[128,2560]{1,0:T(8,128)(2,1)S(1)}, bf16[128,2560]{1,0:T(8,128)(2,1)S(1)}, u32[]{:S(2)}, u32[]{:S(2)}) collective-permute-start(bf16[128,2560]{1,0:T(8,128)(2,1)S(1)} %slice.41), channel_id=1, source_target_pairs={{0,24},{8,0},{16,8},{24,16},{1,25},{9,1},{17,9},{25,17},{2,26},{10... | collective-permute-start | bytes 1966088 | tf_op jit(solution)/shard_map/ppermute | solution.py:147
  89.3 52.2 %all-to-all-start = ((bf16[8,240,1024]{2,1,0:T(8,128)(2,1)}), bf16[8,240,1024]{2,1,0:T(8,128)(2,1)}, u32[]{:S(2)}, u32[]{:S(2)}) async-start(bf16[8,240,1024]{2,1,0:T(8,128)(2,1)} %bitcast.22), calls=%async_computation | async-start | bytes 7864320 | tf_op jit(solution)/shard_map/all_to_all | solution.py:172
  95.7 195.1 %all-gather.12.cloned.1.call-start = ((), (), s32[]{:S(2)}) async-start(), calls=%async_computation.11 | async-start | bytes 3686400 | tf_op jit(solution)/shard_map/all_gather | solution.py:179
  141.5 100.4 %collective-permute-start.4 = (bf16[256,2560]{1,0:T(8,128)(2,1)}, bf16[256,2560]{1,0:T(8,128)(2,1)}, u32[]{:S(2)}, u32[]{:S(2)}) collective-permute-start(bf16[256,2560]{1,0:T(8,128)(2,1)} %get-tuple-element.7), channel_id=1, source_target_pairs={{0,2},{2,4},{4,6},{6,0},{1,3},{3,5},{5,7},{7,1},{8,10},{10,12},{12... | collective-permute-start | bytes 3932168 | tf_op jit(solution)/shard_map/ppermute | solution.py:144
  141.8 101.3 %collective-permute-start.5 = (bf16[256,2560]{1,0:T(8,128)(2,1)}, bf16[256,2560]{1,0:T(8,128)(2,1)}, u32[]{:S(2)}, u32[]{:S(2)}) collective-permute-start(bf16[256,2560]{1,0:T(8,128)(2,1)} %get-tuple-element.7), channel_id=1, source_target_pairs={{0,6},{2,0},{4,2},{6,4},{1,7},{3,1},{5,3},{7,5},{8,14},{10,8},{12,... | collective-permute-start | bytes 3932168 | tf_op jit(solution)/shard_map/ppermute | solution.py:145
  230.5 60.2 %all-to-all-start.1 = ((bf16[8,80,1024]{2,1,0:T(8,128)(2,1)}), bf16[8,80,1024]{2,1,0:T(8,128)(2,1)S(1)}, u32[]{:S(2)}, u32[]{:S(2)}) async-start(bf16[8,80,1024]{2,1,0:T(8,128)(2,1)} %attention.1), calls=%async_computation.1 | async-start | bytes 2621440 | tf_op jit(solution)/shard_map/all_to_all | solution.py:176
  236.8 87.3 %reduce-scatter.4.cloned.1.call-start = ((), (), s32[]{:S(2)}) async-start(), calls=%async_computation.8 | async-start | bytes 2621440 | tf_op jit(solution)/shard_map/reduce_scatter | solution.py:189
  243.0 17.3 %collective-permute-start.6 = (bf16[128,2560]{1,0:T(8,128)(2,1)S(1)}, bf16[128,2560]{1,0:T(8,128)(2,1)S(1)}, u32[]{:S(2)}, u32[]{:S(2)}) collective-permute-start(bf16[128,2560]{1,0:T(8,128)(2,1)S(1)} %slice.42), channel_id=1, source_target_pairs={{0,2},{2,4},{4,6},{6,0},{1,3},{3,5},{5,7},{7,1},{8,10},{10,12},{12... | collective-permute-start | bytes 1966088 | tf_op jit(solution)/shard_map/ppermute | solution.py:146
  244.3 17.0 %collective-permute-start.7 = (bf16[128,2560]{1,0:T(8,128)(2,1)S(1)}, bf16[128,2560]{1,0:T(8,128)(2,1)S(1)}, u32[]{:S(2)}, u32[]{:S(2)}) collective-permute-start(bf16[128,2560]{1,0:T(8,128)(2,1)S(1)} %slice.43), channel_id=1, source_target_pairs={{0,6},{2,0},{4,2},{6,4},{1,7},{3,1},{5,3},{7,5},{8,14},{10,8},{12,... | collective-permute-start | bytes 1966088 | tf_op jit(solution)/shard_map/ppermute | solution.py:147
  295.0 75.3 %reduce-scatter.6.cloned.1.call-start = ((), (), s32[]{:S(2)}) async-start(), calls=%async_computation.9 | async-start | bytes 5242880 | tf_op jit(solution)/shard_map/reduce_scatter | solution.py:189
  309.3 107.3 %reduce-scatter.8.cloned.1.call-start = ((), (), s32[]{:S(2)}) async-start(), calls=%async_computation.10 | async-start | bytes 5242880 | tf_op jit(solution)/shard_map/reduce_scatter | solution.py:189
Sparse Core Ops, SparseCore 0:
  8.9 57.3 all-gather.5
  68.0 67.3 all-gather.7
  137.0 67.4 all-gather.9
  205.9 25.8 all-gather.11
  295.1 28.9 reduce-scatter.3
  326.2 43.9 reduce-scatter.5
  372.6 43.9 reduce-scatter.7

commit v3 on v2

--- a/solution.py
+++ b/solution.py
@@ -9,13 +9,15 @@
 
 LN_EPS = 1e-6
 BF = jnp.bfloat16
+MESH = pl.DeviceIdType.MESH
 F32 = jnp.float32
 TK = 256
 TRIP = 16
 ROWS = 64
 
 
-def attn_kernel(hd, cores, sub, qkv_ref, o_ref, kaug_ref, qaug_ref, m_ref, sa_ref, sb_ref, acc_ref):
+def attn_kernel(hd, side, cores, sub, qkv_ref, x_ref, oin_ref, wide_ref, kaug_ref, qaug_ref, sa_ref, sb_ref, acc_ref, m_ref, o_buf,
+                o_send, o_recv, x_send, x_recv):
     groups, _, toks = qkv_ref.shape
     keys = groups * toks
     bq = sa_ref.shape[1]
@@ -24,10 +26,28 @@
     scale = hd ** -0.5 * math.log2(math.e)
     pad = kaug_ref.shape[1] - 3 * hd
     chunk = TRIP * TK
+    y, core, x = lax.axis_index("y"), lax.axis_index("core"), lax.axis_index("x")
+    me = y * cores + core
+    right, left = (x + 1) % side, (x + side - 1) % side
+    rows = x_ref.shape[0]
+    top, low = pl.ds(0, rows // 2), pl.ds(rows // 2, rows // 2)
+
+    def x_copy(n):
+        src = (x_ref, x_ref, wide_ref.at[3, top], wide_ref.at[1, low])[n]
+        dst = (wide_ref.at[3], wide_ref.at[1], wide_ref.at[2, top], wide_ref.at[2, low])[n]
+        return pltpu.make_async_remote_copy(
+            src_ref=src, dst_ref=dst, send_sem=x_send.at[n], recv_sem=x_recv.at[n],
+            device_id={"x": left if n % 2 else right}, device_id_type=MESH)
+
+    def o_copy(step):
+        to = (me + 1 + step) % groups
+        return pltpu.make_async_remote_copy(
+            src_ref=o_buf.at[step % 2], dst_ref=oin_ref.at[me], send_sem=o_send.at[step % 2], recv_sem=o_recv.at[step],
+            device_id={"y": to // cores, "core": to % cores}, device_id_type=MESH)
 
     def load_query(b, slot):
-        b = jnp.minimum(b, 2 * pl.num_programs(0) - 1)
-        dest, part = b // 2, b % 2
+        b = jnp.minimum(b, 2 * groups - 1)
+        dest, part = (me + 1 + b // 2) % groups, b % 2
         for j in range(subs):
             g = (part * subs + j) * cores + dest % cores
             at = pl.multiple_of((dest // cores) * sub, sub)
@@ -45,6 +65,15 @@
 
     @pl.when(i == 0)
     def _():
+        barrier = pltpu.get_barrier_semaphore()
+        for to in (right, left):
+            pl.semaphore_signal(barrier, inc=1, device_id={"x": to}, device_id_type=MESH)
+        for hop in range(1, groups):
+            to = (me + hop) % groups
+            pl.semaphore_signal(barrier, inc=1, device_id={"y": to // cores, "core": to % cores}, device_id_type=MESH)
+        pl.semaphore_wait(barrier, groups + 1)
+        x_copy(0).start()
+        x_copy(1).start()
         zeros = jnp.zeros((pad, TK), BF)
 
         def spread(t, c):
@@ -66,10 +95,21 @@
             return jnp.maximum(m8, fold(s, jnp.max))
 
         m8 = lax.fori_loop(0, keys // (4 * TK), first, jnp.full((8, bq), -jnp.inf, F32))
-        m_ref[...] = jnp.max(m8, axis=0, keepdims=True)
+        m_ref[...] = jnp.broadcast_to(jnp.max(m8, axis=0, keepdims=True), (8, bq))
+
+    @pl.when(i == groups // 2)
+    def _():
+        x_copy(0).wait()
+        x_copy(1).wait()
+        x_copy(2).start()
+        x_copy(3).start()
+
+    @pl.when(i >= 2)
+    def _():
+        o_copy(i - 2).wait_send()
 
     def half(s_in, s_out, slot, col):
-        m = m_ref[...]
+        m = m_ref[0:1, :]
         acc_ref[...] = jnp.zeros_like(acc_ref)
 
         def trip(c, carry):
@@ -95,38 +135,204 @@
             return m8, l8
 
         m8, l8 = lax.fori_loop(0, keys // chunk, trip, (jnp.full((8, bq), -jnp.inf, F32), jnp.zeros((8, bq), F32)))
-        o_ref[0, :, col:col + bq] = (acc_ref[...] / jnp.sum(l8, axis=0, keepdims=True)).astype(BF)
-        m_ref[...] = jnp.max(m8, axis=0, keepdims=True)
+        o_buf[i % 2, :, col:col + bq] = (acc_ref[...] / jnp.sum(l8, axis=0, keepdims=True)).astype(BF)
+        m_ref[...] = jnp.broadcast_to(jnp.max(m8, axis=0, keepdims=True), (8, bq))
 
     half(sa_ref, sb_ref, 1, 0)
     load_query(2 * i + 2, 0)
     half(sb_ref, sa_ref, 0, bq)
     load_query(2 * i + 3, 1)
 
-
-def attention(qkv, cores, side):
+    @pl.when(i < groups - 1)
+    def _():
+        o_copy(i).start()
+
+    @pl.when(i == groups - 1)
+    def _():
+        own = pltpu.make_async_copy(o_buf.at[i % 2], oin_ref.at[me], o_send.at[i % 2])
+        own.start()
+        x_copy(2).wait()
+        x_copy(3).wait()
+        for step in range(groups - 1):
+            o_copy(step).wait_recv()
+        o_copy(groups - 2).wait_send()
+        own.wait()
+
+
+def attention(qkv, normed, cores, side):
     groups, three, toks = qkv.shape
     hd = three // 3
     keys = groups * toks
     bq = toks // 2
+    anywhere = pl.BlockSpec(memory_space=pl.ANY)
     return pl.pallas_call(
-        functools.partial(attn_kernel, hd, cores, toks // side),
+        functools.partial(attn_kernel, hd, side, cores, toks // side),
         grid=(groups,),
-        in_specs=[pl.BlockSpec((groups, three, toks), lambda i: (0, 0, 0))],
-        out_specs=pl.BlockSpec((1, hd, toks), lambda i: (i, 0, 0)),
-        out_shape=jax.ShapeDtypeStruct((groups, hd, toks), BF),
+        in_specs=[pl.BlockSpec((groups, three, toks), lambda i: (0, 0, 0)), anywhere],
+        out_specs=[anywhere, anywhere],
+        out_shape=[
+            jax.ShapeDtypeStruct((groups, hd, toks), BF),
+            jax.ShapeDtypeStruct((side,) + normed.shape, BF),
+        ],
         scratch_shapes=[
             pltpu.VMEM((keys, 256), BF),
             pltpu.VMEM((2, 256, bq), BF),
-            pltpu.VMEM((1, bq), F32),
             pltpu.VMEM((keys, bq), F32),
             pltpu.VMEM((keys, bq), F32),
             pltpu.VMEM((hd, bq), F32),
+            pltpu.VMEM((8, bq), F32),
+            pltpu.VMEM((2, hd, toks), BF),
+            pltpu.SemaphoreType.DMA((2,)),
+            pltpu.SemaphoreType.DMA((groups - 1,)),
+            pltpu.SemaphoreType.DMA((4,)),
+            pltpu.SemaphoreType.DMA((4,)),
         ],
-        compiler_params=pltpu.CompilerParams(vmem_limit_bytes=58 * 1024 * 1024),
+        compiler_params=pltpu.CompilerParams(vmem_limit_bytes=58 * 1024 * 1024, collective_id=1, has_side_effects=True),
         cost_estimate=pl.CostEstimate(flops=6 * keys * keys * hd, bytes_accessed=8 * keys * hd, transcendentals=keys * keys),
         name="attention",
-    )(qkv)
+    )(qkv, normed)
+
+
+def mlp_kernel(side, x_ref, wide_ref, oin_ref, w1_ref, w2_ref, wo_ref, res_ref, y_ref, w1, w2, xv, xt, ov, hv, part, far, near, res,
+               load, send, recv):
+    x = lax.axis_index("x")
+    right, left = (x + 1) % side, (x + side - 1) % side
+    rows, model = x_ref.shape
+    width = w1_ref.shape[0]
+    heads = wo_ref.shape[0]
+    half = rows // 2
+    top, low = pl.ds(0, half), pl.ds(half, half)
+    order = (2, 1, 3, 0)
+
+    def x_load(n):
+        src = x_ref if order[n] == 0 else wide_ref.at[order[n]]
+        return pltpu.make_async_copy(src, xv.at[n % 2], load.at[n % 2])
+
+    def w1_load(n):
+        cut = pl.ds(n * (width // 2), width // 2)
+        return pltpu.make_async_copy(w1_ref.at[cut], w1.at[cut], load.at[2 + n])
+
+    o_load = pltpu.make_async_copy(oin_ref, ov, load.at[4])
+    w2_load = pltpu.make_async_copy(w2_ref, w2.at[pl.ds(0, width)], load.at[5])
+    wo_load = pltpu.make_async_copy(wo_ref, w2.at[pl.ds(width, heads)], load.at[6])
+    res_load = pltpu.make_async_copy(res_ref, res, load.at[7])
+    x_load(0).start()
+    w1_load(0).start()
+    w1_load(1).start()
+    o_load.start()
+    w2_load.start()
+    wo_load.start()
+    x_load(1).start()
+    res_load.start()
+
+    barrier = pltpu.get_barrier_semaphore()
+    for to in (right, left):
+        pl.semaphore_signal(barrier, inc=1, device_id={"x": to}, device_id_type=MESH)
+    pl.semaphore_wait(barrier, 2)
+
+    def put(n, src, dst, to):
+        return pltpu.make_async_remote_copy(src_ref=src, dst_ref=dst, send_sem=send.at[n], recv_sem=recv.at[n],
+                                            device_id={"x": to}, device_id_type=MESH)
+
+    puts = (
+        put(0, part.at[0, top], far.at[0], right),
+        put(1, part.at[0, low], far.at[1], left),
+        put(2, part.at[1, low], near.at[0, low], right),
+        put(3, part.at[2, top], near.at[1, top], left),
+        put(4, part.at[1, top], near.at[0, top], right),
+        put(5, part.at[2, low], near.at[1, low], left),
+    )
+
+    def compute(n, slot):
+        x_load(n).wait()
+
+        def flip(k, c):
+            at = pl.ds(pl.multiple_of(k * 256, 256), 256)
+            xt[at, :] = xv[n % 2, :, at].T
+            return c
+
+        lax.fori_loop(0, model // 256, flip, 0, unroll=2)
+        hd, toks = ov.shape[1:]
+        col = pl.multiple_of((x + order[n]) % side * rows, rows)
+        if n == 0:
+            o_load.wait()
+        hv[:, width:] = ov[:, :, pl.ds(col, rows)].reshape(heads, rows).T
+
+        def hidden(f, c):
+            at = pl.ds(pl.multiple_of(f * 512, 512), 512)
+            pre = jnp.dot(w1[at, :], xt[...], preferred_element_type=F32)
+            hv[:, at] = jax.nn.gelu(pre, approximate=True).astype(BF).T
+            return c
+
+        if n == 0:
+            w1_load(0).wait()
+            w1_load(1).wait()
+        lax.fori_loop(0, width // 512, hidden, 0)
+        if n < 2:
+            x_load(n + 2).start()
+        if n == 0:
+            w2_load.wait()
+            wo_load.wait()
+
+        def outs(d, c):
+            at = pl.ds(pl.multiple_of(d * 512, 512), 512)
+            part[slot, :, at] = jnp.dot(hv[...], w2[:, at], preferred_element_type=F32)
+            return c
+
+        lax.fori_loop(0, model // 512, outs, 0)
+
+    compute(0, 0)
+    puts[0].start()
+    puts[1].start()
+    compute(1, 1)
+    puts[2].start()
+    compute(2, 2)
+    puts[3].start()
+    puts[0].wait()
+    part[1, :half, :] += far[0]
+    puts[4].start()
+    puts[1].wait()
+    part[2, half:, :] += far[1]
+    puts[5].start()
+    compute(3, 0)
+    res_load.wait()
+    part[0] += res[...].astype(F32)
+    puts[2].wait()
+    puts[3].wait()
+    puts[4].wait()
+    puts[5].wait()
+    y_ref[...] = (part[0] + near[0] + near[1]).astype(BF)
+
+
+def mlp(x_loc, normed, wide, oin, w1, w2, wo, side):
+    rows, model = normed.shape
+    width = w1.shape[0]
+    anywhere = pl.BlockSpec(memory_space=pl.ANY)
+    flops = 2 * side * rows * model * (2 * width + wo.shape[0])
+    return pl.pallas_call(
+        functools.partial(mlp_kernel, side),
+        in_specs=[anywhere] * 7,
+        out_specs=pl.BlockSpec(memory_space=pltpu.VMEM),
+        out_shape=jax.ShapeDtypeStruct((rows, model), BF),
+        scratch_shapes=[
+            pltpu.VMEM(w1.shape, BF),
+            pltpu.VMEM((width + wo.shape[0], model), BF),
+            pltpu.VMEM((2, rows, model), BF),
+            pltpu.VMEM((model, rows), BF),
+            pltpu.VMEM(oin.shape, BF),
+            pltpu.VMEM((rows, width + wo.shape[0]), BF),
+            pltpu.VMEM((3, rows, model), F32),
+            pltpu.VMEM((2, rows // 2, model), F32),
+            pltpu.VMEM((2, rows, model), F32),
+            pltpu.VMEM((rows, model), BF),
+            pltpu.SemaphoreType.DMA((8,)),
+            pltpu.SemaphoreType.DMA((6,)),
+            pltpu.SemaphoreType.DMA((6,)),
+        ],
+        compiler_params=pltpu.CompilerParams(vmem_limit_bytes=62 * 1024 * 1024, collective_id=2, has_side_effects=True),
+        cost_estimate=pl.CostEstimate(flops=flops, bytes_accessed=4 * model * width, transcendentals=side * rows * width),
+        name="mlp",
+    )(normed, wide, oin, w1, w2, wo, x_loc)
 
 
 def layer_norm(row_vals, ln_gain):
@@ -163,31 +369,17 @@
     row, col = ("x", "core"), ("y", "core")
 
     def local_block(x_loc, ln_gamma, w_qkv, w_out, w_up, w_down):
-        residual = x_loc.astype(F32)
-        normed = layer_norm(residual, ln_gamma)
+        normed = layer_norm(x_loc.astype(F32), ln_gamma)
         wqkv = lax.all_gather(w_qkv[:, 0, :].T, row, axis=0, tiled=True)
         tall = ring_gather(normed, "y", side)
         qkv = lax.dot_general(wqkv, tall, (((1,), (1,)), ((), ())), preferred_element_type=F32).astype(BF)
         qkv = qkv.reshape(side * cores, -1, tall.shape[0])
         qkv = lax.all_to_all(qkv, row, split_axis=0, concat_axis=0, tiled=True)
-        qkv, normed = lax.optimization_barrier((qkv, normed))
-        wide = ring_gather(normed, "x", side)
-        out = attention(qkv, cores, side)
-        out = lax.all_to_all(out, col, split_axis=0, concat_axis=0, tiled=True)
-        out = out.reshape(-1, out.shape[2])
+        oin, wide = attention(qkv, normed, cores, side)
         wup = lax.all_gather(w_up.T, col, axis=0, tiled=True)
         wout = lax.all_gather(w_out[0], col, axis=0, tiled=True)
         wdown = lax.all_gather(w_down, col, axis=0, tiled=True)
-        pre = lax.dot_general(wide, wup, (((1,), (1,)), ((), ())), preferred_element_type=F32)
-        hidden = jax.nn.gelu(pre, approximate=True).astype(BF)
-        width = wdown.shape[1]
-        cuts = [0, width // 5, 3 * width // 5, width]
-        reduced = []
-        for a, b in zip(cuts[:-1], cuts[1:]):
-            part = jnp.dot(hidden, wdown[:, a:b], preferred_element_type=F32)
-            part = part + lax.dot_general(out, wout[:, a:b], (((0,), (0,)), ((), ())), preferred_element_type=F32)
-            reduced.append(lax.psum_scatter(part, "x", scatter_dimension=0, tiled=True))
-        return (residual + jnp.concatenate(reduced, axis=1)).astype(BF)
+        return mlp(x_loc, normed, wide, oin, wup, wdown, wout, side)
 
     row_spec = P(("data", "y", "x", "core"), None)
     tp_axes = ("y", "x", "core")

time: 427 us -> 359 us (0.84)
  waiting for transfers between devices: 187 us -> 59.9 us
  Pallas kernels: 86.4 us -> 191 us
  matrix products: 77.6 us -> 16.5 us
  blocking collectives: 0 us -> 52 us
  starting transfers between devices: 26.6 us -> 8.21 us
  local copies, waits for them, and re-layouts: 29.5 us -> 15.6 us
    pallas_call x1 -> x2, Pallas kernels: 86.4 us -> 191 us  [the longest x1 105 us: mlp(): pl.pallas_call(functools.partial(mlp_kernel, side), in_specs=[anywhere] *...]
    reduce_scatter x3 -> x0, waiting for transfers between devices: 92.8 us -> none  [local_block(): reduced.append(lax.psum_scatter(part, 'x', scatter_dimension=0, tiled=True))]
    dot_general x7 -> x0, matrix products: 61.1 us -> none  [the longest x3 25.6 us: local_block(): part = jnp.dot(hidden, wdown[:, a:b], preferred_element_type=F32)]
    all_to_all x0 -> x1, blocking collectives: none -> 52 us  [local_block(): qkv = lax.all_to_all(qkv, row, split_axis=0, concat_axis=0, tiled=True)]
    all_to_all x2 -> x0, waiting for transfers between devices: 45.1 us -> none  [the longest x1 45.1 us: local_block(): qkv = lax.all_to_all(qkv, row, split_axis=0, concat_axis=0, tiled=True)]
    all_gather x1, waiting for transfers between devices: 0.01 us -> 17.1 us  [local_block(): wup = lax.all_gather(w_up.T, col, axis=0, tiled=True)]
    all_to_all x2 -> x0, starting transfers between devices: 12.7 us -> none  [the longest x1 6.41 us: local_block(): qkv = lax.all_to_all(qkv, row, split_axis=0, concat_axis=0, tiled=True)]
    dynamic_update_slice x9 -> x4, local copies, waits for them, and re-layouts: 14.6 us -> 4.04 us  [ring_gather(): lax.dynamic_update_slice(full, part, (pos % side * rows + off, 0))]
  transfers between devices with their start and end apart: 17 -> 8, of which waited for: 7 -> 3; matrix products, arithmetic and copies ran while one was open for 25% -> 8% of each run, Pallas kernels for 20% -> 24%
where the time goes in v3:
time: 359 us; the launch traced here: 358 us
  Pallas kernels  191 us (53%)
  waiting for transfers between devices  59.9 us (17%)
  blocking collectives  52 us (14%)
  matrix products  16.5 us (5%)
  local copies, waits for them, and re-layouts  15.6 us (4%)
  between operations  13.3 us (4%)
  starting transfers between devices  8.21 us (2%)
    pallas_call x1, Pallas kernels, mlp(): pl.pallas_call(functools.partial(mlp_kernel, side), in_specs=[anywhere] *...  105 us
    pallas_call x1, Pallas kernels, attention(): pl.pallas_call(functools.partial(attn_kernel, hd, side, cores, toks // si...  86.1 us
    all_to_all x1, blocking collectives, local_block(): qkv = lax.all_to_all(qkv, row, split_axis=0, concat_axis=0, tiled=True)  52 us
    ppermute x1, waiting for transfers between devices, ring_gather(): before = lax.ppermute(block, axis, up)  28.6 us
    all_gather x1, waiting for transfers between devices, local_block(): wup = lax.all_gather(w_up.T, col, axis=0, tiled=True)  17.1 us
    dot_general x1, matrix products, local_block(): lax.dot_general(wqkv, tall, (((1,), (1,)), ((), ())), preferred_element_t...  16.5 us
    ppermute x1, waiting for transfers between devices, ring_gather(): far_a = lax.ppermute(before[:half], axis, up)  11.3 us
  transfers between devices with their start and end apart: 8, of which 3 were waited for; matrix products, arithmetic and copies ran while one was open for 8% of the time, Pallas kernels for 24%

profile of v3, /device:TPU:97, one launch (start us, length us, event | category | flops | bytes accessed | tf_op | source)
XLA Modules:
  0.0 358.5 jit_solution(13493164306257141311)
XLA Ops:
  6.6 0.7 all-gather.6.cloned.1.call-update
  7.4 0.7 all-gather.12.cloned.1.call-update
  8.2 0.7 all-gather.10.cloned.1.call-update
  9.0 0.6 all-gather.8.cloned.1.call-update
  9.9 0.5 fusion.2
  10.4 0.3 broadcast_in_dim.2
  10.7 1.6 constant_dynamic-update-slice_fusion.4
  12.3 2.3 copy-done.1
  14.5 2.7 collective-permute-start
  17.2 2.5 collective-permute-start.1
  19.7 28.6 %collective-permute-done = bf16[256,2560]{1,0:T(8,128)(2,1)S(1)} collective-permute-done((bf16[256,2560]{1,0:T(8,128)(2,1)}, bf16[256,2560]{1,0:T(8,128)(2,1)S(1)}, u32[]{:S(2)}, u32[]{:S(2)}) %collective-permute-start) | collective-permute-done | bytes 1310752 | tf_op jit(solution)/shard_map/ppermute | solution.py:350
  48.6 2.7 collective-permute-start.3
  51.3 1.1 constant_dynamic-update-slice_fusion.3
  52.5 1.1 constant_dynamic-update-slice_fusion.2
  53.6 11.3 %collective-permute-done.2 = bf16[128,2560]{1,0:T(8,128)(2,1)S(1)} collective-permute-done((bf16[128,2560]{1,0:T(8,128)(2,1)S(1)}, bf16[128,2560]{1,0:T(8,128)(2,1)S(1)}, u32[]{:S(2)}, u32[]{:S(2)}) %collective-permute-start.2) | collective-permute-done | bytes 655392 | tf_op jit(solution)/shard_map/ppermute | solution.py:352
  64.9 0.9 constant_dynamic-update-slice_fusion.1
  65.8 0.9 constant_dynamic-update-slice_fusion
  66.7 16.5 %convert_bitcast_fusion = bf16[1920,1024]{0,1:T(8,128)(2,1)} fusion(bf16[1024,2560]{1,0:T(8,128)(2,1)} %constant_dynamic-update-slice_fusion, bf16[1920,2560]{1,0:T(8,128)(2,1)} %all-gather.6.cloned.1.call-done), kind=kOutput, calls=%fused_computation | convolution fusion | flops 10068295680 | bytes 19005440 | tf_op jit(solution)/shard_map/dot_general | solution.py:375
  83.3 6.4 %copy.7 = bf16[1920,1024]{1,0:T(8,128)(2,1)} copy(bf16[1920,1024]{0,1:T(8,128)(2,1)} %convert_bitcast_fusion) | data formatting | bytes 7864320 | tf_op jit(solution)/shard_map/convert_element_type | solution.py:375
  89.6 52.0 %all_to_all.5.qkv_ref = bf16[8,240,1024]{2,1,0:T(8,128)(2,1)} all-to-all(bf16[8,240,1024]{2,1,0:T(8,128)(2,1)} %bitcast.10), channel_id=1, replica_groups=mesh['data'=1,'y'=4,'x'=4,'core'=2] {'x','core'}, dimensions={0} | all-to-all | bytes 7864320 | tf_op jit(solution)/shard_map/all_to_all | solution.py:377
  141.6 86.1 %attention.1 = (bf16[8,80,1024]{2,1,0:T(8,128)(2,1)}, bf16[4,256,2560]{2,1,0:T(8,128)(2,1)}) custom-call(bf16[8,240,1024]{2,1,0:T(8,128)(2,1)} %all_to_all.5.qkv_ref, bf16[256,2560]{1,0:T(8,128)(2,1)} %get-tuple-element.10.x_ref), custom_call_target="tpu_custom_call" | custom-call | flops 32212254720 | bytes 5242880 | tf_op jit(solution)/shard_map/attention/pallas_call | solution.py:168
  227.8 17.1 %all-gather.8.cloned.1.call-done.w1_ref = bf16[2560,2560]{1,0:T(8,128)(2,1)} async-done(((bf16[320,2560]{1,0:T(8,128)(2,1)}), bf16[2560,2560]{1,0:T(8,128)(2,1)}) %all-gather.8.cloned.1.call-update) | async-done | bytes 13107216 | tf_op jit(solution)/shard_map/all_gather | solution.py:379
  244.8 104.6 %mlp.1 = bf16[256,2560]{1,0:T(8,128)(2,1)} custom-call(bf16[256,2560]{1,0:T(8,128)(2,1)} %get-tuple-element.10.x_ref, bf16[4,256,2560]{2,1,0:T(8,128)(2,1)} %get-tuple-element.7.wide_ref, bf16[8,80,1024]{2,1,0:T(8,128)(2,1)} %get-tuple-element.8.oin_ref, bf16[2560,2560]{1,0:T(8,128)(2,1)} %all-gather.8.cloned.1.call-done.w1_ref, ...), custom_call_target="tpu_custom_call" | custom-call | flops 30198988800 | bytes 26214400 | tf_op jit(solution)/shard_map/mlp/pallas_call | solution.py:312
  349.5 2.5 copy.14
  (20 shorter events, 0.7 us)
Async XLA Ops:
  6.5 3.0 copy-start
  6.5 60.2 %all-gather.6.cloned.1.call-start = ((), (), s32[]{:S(2)}) async-start(), calls=%async_computation.1 | async-start | bytes 11059200 | tf_op jit(solution)/shard_map/all_gather | solution.py:373
  7.3 220.4 %all-gather.12.cloned.1.call-start = ((), (), s32[]{:S(2)}) async-start(), calls=%async_computation.4 | async-start | bytes 3686400 | tf_op jit(solution)/shard_map/all_gather | solution.py:380
  8.1 219.6 %all-gather.10.cloned.1.call-start = ((), (), s32[]{:S(2)}) async-start(), calls=%async_computation.3 | async-start | bytes 14745600 | tf_op jit(solution)/shard_map/all_gather | solution.py:381
  8.9 235.9 %all-gather.8.cloned.1.call-start = ((), (), s32[]{:S(2)}) async-start(), calls=%async_computation.2 | async-start | bytes 14745600 | tf_op jit(solution)/shard_map/all_gather | solution.py:379
  9.6 1.1 copy-start.2
  12.3 2.3 copy-start.1
  14.5 33.8 %collective-permute-start = (bf16[256,2560]{1,0:T(8,128)(2,1)}, bf16[256,2560]{1,0:T(8,128)(2,1)S(1)}, u32[]{:S(2)}, u32[]{:S(2)}) collective-permute-start(bf16[256,2560]{1,0:T(8,128)(2,1)} %get-tuple-element.10.x_ref), channel_id=1, source_target_pairs={{0,8},{8,16},{16,24},{24,0},{1,9},{9,17},{17,25},{25,1},{2,10},{10... | collective-permute-start | bytes 3932168 | tf_op jit(solution)/shard_map/ppermute | solution.py:350
  17.2 31.3 %collective-permute-start.1 = (bf16[256,2560]{1,0:T(8,128)(2,1)}, bf16[256,2560]{1,0:T(8,128)(2,1)S(1)}, u32[]{:S(2)}, u32[]{:S(2)}) collective-permute-start(bf16[256,2560]{1,0:T(8,128)(2,1)} %get-tuple-element.10.x_ref), channel_id=1, source_target_pairs={{0,24},{8,0},{16,8},{24,16},{1,25},{9,1},{17,9},{25,17},{2,26},{10... | collective-permute-start | bytes 3932168 | tf_op jit(solution)/shard_map/ppermute | solution.py:351
  48.4 16.5 %collective-permute-start.2 = (bf16[128,2560]{1,0:T(8,128)(2,1)S(1)}, bf16[128,2560]{1,0:T(8,128)(2,1)S(1)}, u32[]{:S(2)}, u32[]{:S(2)}) collective-permute-start(bf16[128,2560]{1,0:T(8,128)(2,1)S(1)} %slice.8), channel_id=1, source_target_pairs={{0,8},{8,16},{16,24},{24,0},{1,9},{9,17},{17,25},{25,1},{2,10},{10... | collective-permute-start | bytes 1966088 | tf_op jit(solution)/shard_map/ppermute | solution.py:352
  48.6 17.2 %collective-permute-start.3 = (bf16[128,2560]{1,0:T(8,128)(2,1)S(1)}, bf16[128,2560]{1,0:T(8,128)(2,1)S(1)}, u32[]{:S(2)}, u32[]{:S(2)}) collective-permute-start(bf16[128,2560]{1,0:T(8,128)(2,1)S(1)} %slice.9), channel_id=1, source_target_pairs={{0,24},{8,0},{16,8},{24,16},{1,25},{9,1},{17,9},{25,17},{2,26},{10... | collective-permute-start | bytes 1966088 | tf_op jit(solution)/shard_map/ppermute | solution.py:353
Sparse Core Ops, SparseCore 0:
  8.9 57.3 all-gather.5
  68.0 25.8 all-gather.11
  95.4 67.0 all-gather.9
  164.0 80.8 all-gather.7

commit v4 on v3

--- a/solution.py
+++ b/solution.py
@@ -16,8 +16,205 @@
 ROWS = 64
 
 
-def attn_kernel(hd, side, cores, sub, qkv_ref, x_ref, oin_ref, wide_ref, kaug_ref, qaug_ref, sa_ref, sb_ref, acc_ref, m_ref, o_buf,
-                o_send, o_recv, x_send, x_recv):
+def ring(own, full, axis, split, send, recv):
+    side, cores = lax.axis_size(axis), lax.axis_size("core")
+    at, core = lax.axis_index(axis), lax.axis_index("core")
+    other = (core + 1) % cores
+    block = lambda hop: full.at[(at + hop) % side * cores + core]
+    head, tail = pl.ds(0, split), pl.ds(split, own.shape[0] - split)
+    nxt, prv, sib = {axis: (at + 1) % side}, {axis: (at + side - 1) % side}, {"core": other}
+    plan = (
+        (own, block(0), nxt),
+        (own, block(0), prv),
+        (own, block(0), sib),
+        (block(side - 1).at[head], block(side - 1).at[head], nxt),
+        (block(1).at[tail], block(1).at[tail], prv),
+        (block(side - 1), block(side - 1), sib),
+        (block(1), block(1), sib),
+        (block(2), block(2), sib),
+    )
+    return [
+        pltpu.make_async_remote_copy(
+            src_ref=src, dst_ref=dst, send_sem=send.at[n], recv_sem=recv.at[n], device_id=to, device_id_type=MESH)
+        for n, (src, dst, to) in enumerate(plan)
+    ]
+
+
+def start(copies, *which):
+    for n in which:
+        copies[n].start()
+
+
+def arrived(copies, *which):
+    for n in which:
+        copies[n].wait_recv()
+
+
+def meet(*places):
+    barrier = pltpu.get_barrier_semaphore()
+    for place in places:
+        pl.semaphore_signal(barrier, inc=1, device_id=place, device_id_type=MESH)
+    pl.semaphore_wait(barrier, len(places))
+
+
+def qkv_kernel(side, cores, x_ref, gain_ref, wq_ref, w1_ref, qkv_ref, normed_ref, w1_full, wv, xv, xt, qk,
+               wq_send, wq_recv, x_send, x_recv, w1_send, w1_recv, a_send, a_recv, local):
+    y, x, core = lax.axis_index("y"), lax.axis_index("x"), lax.axis_index("core")
+    rows, model = x_ref.shape
+    low = rows // 2
+    me = x * cores + core
+    up, down = {"y": (y + 1) % side}, {"y": (y + side - 1) % side}
+    meet(up, down, *[
+        {"x": (x + dx) % side, "core": (core + dc) % cores} for dx in range(side) for dc in range(cores) if dx or dc])
+
+    wq = ring(wq_ref, wv, "x", wq_ref.shape[0] // 32 * 16, wq_send, wq_recv)
+    w1 = ring(w1_ref, w1_full, "y", w1_ref.shape[0] // 2, w1_send, w1_recv)
+    own_wq = pltpu.make_async_copy(wq_ref, wv.at[me], local.at[0])
+    own_wq.start()
+    start(wq, 0, 1, 2)
+
+    def x_copy(n, src, to):
+        return pltpu.make_async_remote_copy(
+            src_ref=src, dst_ref=src, send_sem=x_send.at[n], recv_sem=x_recv.at[n], device_id=to, device_id_type=MESH)
+
+    before, after, far = (y + side - 1) % side, (y + 1) % side, (y + 2) % side
+    xs = [
+        x_copy(0, xv.at[y], up),
+        x_copy(1, xv.at[y], down),
+        x_copy(2, xv.at[before, pl.ds(0, low)], up),
+        x_copy(3, xv.at[after, pl.ds(low, low)], down),
+    ]
+
+    def norm(r, c):
+        at = pl.ds(pl.multiple_of(r * 32, 32), 32)
+        row = x_ref[at, :].astype(F32)
+        mean = jnp.mean(row, axis=-1, keepdims=True)
+        centered = row - mean
+        var = jnp.mean(centered * centered, axis=-1, keepdims=True)
+        xv[y, at, :] = (centered * lax.rsqrt(var + LN_EPS) * gain_ref[...]).astype(BF)
+        return c
+
+    lax.fori_loop(0, rows // 32, norm, 0)
+
+    def cols(part):
+        return pl.ds(pl.multiple_of(part * rows, rows), rows)
+
+    def flip(part):
+        def piece(k, c):
+            at = pl.ds(pl.multiple_of(k * 256, 256), 256)
+            xt[at, cols(part)] = xv[part, :, at].T
+            return c
+
+        lax.fori_loop(0, model // 256, piece, 0, unroll=2)
+
+    flip(y)
+    start(xs, 0, 1)
+    start(w1, 2, 0, 1)
+    keep = pltpu.make_async_copy(xv.at[y], normed_ref, local.at[1])
+    keep.start()
+
+    def unit(head, part):
+        qk[head, :, cols(part)] = jnp.dot(wv[head], xt[:, cols(part)], preferred_element_type=F32).astype(BF)
+
+    def send(n, head):
+        return pltpu.make_async_remote_copy(
+            src_ref=qk.at[head], dst_ref=qkv_ref.at[me], send_sem=a_send.at[n], recv_sem=a_recv.at[n],
+            device_id={"x": head // cores, "core": head % cores}, device_id_type=MESH)
+
+    def head_of(n):
+        return (x + n // cores) % side * cores + (core + n) % cores
+
+    arrived(wq, 0, 1)
+    start(wq, 3, 4, 5, 6)
+    arrived(xs, 0, 1)
+    start(xs, 2, 3)
+    flip(before)
+    flip(after)
+    own_wq.wait()
+    arrived(wq, 2, 5, 6)
+
+    def near(k, c):
+        n, p = k // 3, k % 3
+        n = n + cores * (n // (2 * cores))
+        unit(head_of(n), (y + p + p // 2) % side)
+        return c
+
+    lax.fori_loop(0, 3 * 3 * cores, near, 0)
+    arrived(wq, 3, 4)
+    start(wq, 7)
+    arrived(xs, 2, 3)
+    flip(far)
+
+    def close(k, c):
+        n = cores * (1 + 2 * (k // cores)) + k % cores
+        unit(head_of(n), far)
+        send(n, head_of(n)).start()
+        return c
+
+    lax.fori_loop(0, 2 * cores, close, 0)
+    arrived(wq, 7)
+
+    def distant(k, c):
+        unit(head_of(2 * cores + k // side), k % side)
+        return c
+
+    for k in range(cores):
+        lax.fori_loop(k * side, (k + 1) * side, distant, 0)
+        send(2 * cores + k, head_of(2 * cores + k)).start()
+
+    def home(k, c):
+        unit(head_of(k), far)
+        return c
+
+    lax.fori_loop(0, cores, home, 0)
+    for n in range(1, cores):
+        send(n, head_of(n)).start()
+    own = pltpu.make_async_copy(qk.at[me], qkv_ref.at[me], local.at[2])
+    own.start()
+    arrived(w1, 0, 1)
+    start(w1, 3, 4, 5, 6)
+    for n in range(1, side * cores):
+        send(n, head_of(n)).wait()
+    own.wait()
+    keep.wait()
+    arrived(w1, 3, 4)
+    start(w1, 7)
+    arrived(w1, 2, 5, 6, 7)
+    for copies in (wq, w1, xs):
+        for copy in copies:
+            copy.wait_send()
+
+
+def qkv_stage(x_loc, gain, wq, w1, cores, side):
+    rows, model = x_loc.shape
+    groups = side * cores
+    anywhere = pl.BlockSpec(memory_space=pl.ANY)
+    vmem = pl.BlockSpec(memory_space=pltpu.VMEM)
+    dma = lambda n: pltpu.SemaphoreType.DMA((n,))
+    return pl.pallas_call(
+        functools.partial(qkv_kernel, side, cores),
+        in_specs=[vmem, vmem, anywhere, anywhere],
+        out_specs=[anywhere] * 3,
+        out_shape=[
+            jax.ShapeDtypeStruct((groups, wq.shape[0], side * rows), BF),
+            jax.ShapeDtypeStruct((rows, model), BF),
+            jax.ShapeDtypeStruct((groups,) + w1.shape, BF),
+        ],
+        scratch_shapes=[
+            pltpu.VMEM((groups,) + wq.shape, BF),
+            pltpu.VMEM((side, rows, model), BF),
+            pltpu.VMEM((model, side * rows), BF),
+            pltpu.VMEM((groups, wq.shape[0], side * rows), BF),
+            dma(8), dma(8), dma(4), dma(4), dma(8), dma(8), dma(groups), dma(groups), dma(3),
+        ],
+        compiler_params=pltpu.CompilerParams(vmem_limit_bytes=48 * 1024 * 1024, collective_id=0, has_side_effects=True),
+        cost_estimate=pl.CostEstimate(flops=2 * side * rows * model * groups * wq.shape[0], bytes_accessed=4 * w1.size, transcendentals=0),
+        name="qkv",
+    )(x_loc, gain, wq, w1)
+
+
+def attn_kernel(hd, side, cores, sub, qkv_ref, x_ref, w2_ref, wo_ref, oin_ref, wide_ref, w2_full, wo_full, kaug_ref, qaug_ref, sa_ref,
+                sb_ref, acc_ref, m_ref, o_buf, o_send, o_recv, x_send, x_recv, w2_send, w2_recv, wo_send, wo_recv):
     groups, _, toks = qkv_ref.shape
     keys = groups * toks
     bq = sa_ref.shape[1]
@@ -44,6 +241,9 @@
         return pltpu.make_async_remote_copy(
             src_ref=o_buf.at[step % 2], dst_ref=oin_ref.at[me], send_sem=o_send.at[step % 2], recv_sem=o_recv.at[step],
             device_id={"y": to // cores, "core": to % cores}, device_id_type=MESH)
+
+    w2 = ring(w2_ref, w2_full, "y", w2_ref.shape[0] // 2, w2_send, w2_recv)
+    wo = ring(wo_ref, wo_full, "y", wo_ref.shape[0] // 32 * 16, wo_send, wo_recv)
 
     def load_query(b, slot):
         b = jnp.minimum(b, 2 * groups - 1)
@@ -65,13 +265,10 @@
 
     @pl.when(i == 0)
     def _():
-        barrier = pltpu.get_barrier_semaphore()
-        for to in (right, left):
-            pl.semaphore_signal(barrier, inc=1, device_id={"x": to}, device_id_type=MESH)
-        for hop in range(1, groups):
-            to = (me + hop) % groups
-            pl.semaphore_signal(barrier, inc=1, device_id={"y": to // cores, "core": to % cores}, device_id_type=MESH)
-        pl.semaphore_wait(barrier, groups + 1)
+        meet({"x": right}, {"x": left}, *[
+            {"y": (me + hop) % groups // cores, "core": (me + hop) % cores} for hop in range(1, groups)])
+        start(wo, 0, 1, 2)
+        start(w2, 0, 1, 2)
         x_copy(0).start()
         x_copy(1).start()
         zeros = jnp.zeros((pad, TK), BF)
@@ -103,6 +300,15 @@
         x_copy(1).wait()
         x_copy(2).start()
         x_copy(3).start()
+        for copies in (wo, w2):
+            arrived(copies, 0, 1)
+            start(copies, 3, 4, 5, 6)
+
+    @pl.when(i == groups - 1)
+    def _():
+        for copies in (wo, w2):
+            arrived(copies, 3, 4)
+            start(copies, 7)
 
     @pl.when(i >= 2)
     def _():
@@ -157,9 +363,13 @@
             o_copy(step).wait_recv()
         o_copy(groups - 2).wait_send()
         own.wait()
-
-
-def attention(qkv, normed, cores, side):
+        for copies in (wo, w2):
+            arrived(copies, 2, 5, 6, 7)
+            for copy in copies:
+                copy.wait_send()
+
+
+def attention(qkv, normed, w2, wo, cores, side):
     groups, three, toks = qkv.shape
     hd = three // 3
     keys = groups * toks
@@ -168,11 +378,13 @@
     return pl.pallas_call(
         functools.partial(attn_kernel, hd, side, cores, toks // side),
         grid=(groups,),
-        in_specs=[pl.BlockSpec((groups, three, toks), lambda i: (0, 0, 0)), anywhere],
-        out_specs=[anywhere, anywhere],
+        in_specs=[pl.BlockSpec((groups, three, toks), lambda i: (0, 0, 0)), anywhere, anywhere, anywhere],
+        out_specs=[anywhere] * 4,
         out_shape=[
             jax.ShapeDtypeStruct((groups, hd, toks), BF),
             jax.ShapeDtypeStruct((side,) + normed.shape, BF),
+            jax.ShapeDtypeStruct((groups,) + w2.shape, BF),
+            jax.ShapeDtypeStruct((groups,) + wo.shape, BF),
         ],
         scratch_shapes=[
             pltpu.VMEM((keys, 256), BF),
@@ -186,21 +398,27 @@
             pltpu.SemaphoreType.DMA((groups - 1,)),
             pltpu.SemaphoreType.DMA((4,)),
             pltpu.SemaphoreType.DMA((4,)),
+            pltpu.SemaphoreType.DMA((8,)),
+            pltpu.SemaphoreType.DMA((8,)),
+            pltpu.SemaphoreType.DMA((8,)),
+            pltpu.SemaphoreType.DMA((8,)),
         ],
         compiler_params=pltpu.CompilerParams(vmem_limit_bytes=58 * 1024 * 1024, collective_id=1, has_side_effects=True),
         cost_estimate=pl.CostEstimate(flops=6 * keys * keys * hd, bytes_accessed=8 * keys * hd, transcendentals=keys * keys),
         name="attention",
-    )(qkv, normed)
-
-
-def mlp_kernel(side, x_ref, wide_ref, oin_ref, w1_ref, w2_ref, wo_ref, res_ref, y_ref, w1, w2, xv, xt, ov, hv, part, far, near, res,
-               load, send, recv):
+    )(qkv, normed, w2, wo)
+
+
+def mlp_kernel(side, cores, x_ref, wide_ref, oin_ref, w1_own, w2_own, wo_own, w1_ref, w2_ref, wo_ref, res_ref, y_ref, w1, w2, xv, xt, ov,
+               hv, part, far, near, res, load, send, recv):
     x = lax.axis_index("x")
     right, left = (x + 1) % side, (x + side - 1) % side
     rows, model = x_ref.shape
-    width = w1_ref.shape[0]
-    heads = wo_ref.shape[0]
+    groups = w1_ref.shape[0]
+    width = groups * w1_own.shape[0]
+    heads = groups * wo_own.shape[0]
     half = rows // 2
+    me = lax.axis_index("y") * cores + lax.axis_index("core")
     top, low = pl.ds(0, half), pl.ds(half, half)
     order = (2, 1, 3, 0)
 
@@ -208,27 +426,25 @@
         src = x_ref if order[n] == 0 else wide_ref.at[order[n]]
         return pltpu.make_async_copy(src, xv.at[n % 2], load.at[n % 2])
 
-    def w1_load(n):
-        cut = pl.ds(n * (width // 2), width // 2)
-        return pltpu.make_async_copy(w1_ref.at[cut], w1.at[cut], load.at[2 + n])
-
-    o_load = pltpu.make_async_copy(oin_ref, ov, load.at[4])
-    w2_load = pltpu.make_async_copy(w2_ref, w2.at[pl.ds(0, width)], load.at[5])
-    wo_load = pltpu.make_async_copy(wo_ref, w2.at[pl.ds(width, heads)], load.at[6])
-    res_load = pltpu.make_async_copy(res_ref, res, load.at[7])
+    def gathered(own, full, into, base, sem):
+        size = own.shape[0]
+        for hop in range(groups):
+            slot = (me + hop) % groups
+            to = into.at[pl.ds(pl.multiple_of(base + slot * size, 16), size)]
+            pltpu.make_async_copy(full.at[slot] if hop else own, to, sem).start()
+        whole = into.at[pl.ds(base, groups * size)]
+        return pltpu.make_async_copy(whole, whole, sem)
+
+    o_load = pltpu.make_async_copy(oin_ref, ov, load.at[2])
+    res_load = pltpu.make_async_copy(res_ref, res, load.at[3])
     x_load(0).start()
-    w1_load(0).start()
-    w1_load(1).start()
+    w1_load = gathered(w1_own, w1_ref, w1, 0, load.at[4])
     o_load.start()
-    w2_load.start()
-    wo_load.start()
+    w2_load = gathered(w2_own, w2_ref, w2, 0, load.at[5])
+    wo_load = gathered(wo_own, wo_ref, w2, width, load.at[6])
     x_load(1).start()
     res_load.start()
-
-    barrier = pltpu.get_barrier_semaphore()
-    for to in (right, left):
-        pl.semaphore_signal(barrier, inc=1, device_id={"x": to}, device_id_type=MESH)
-    pl.semaphore_wait(barrier, 2)
+    meet({"x": right}, {"x": left})
 
     def put(n, src, dst, to):
         return pltpu.make_async_remote_copy(src_ref=src, dst_ref=dst, send_sem=send.at[n], recv_sem=recv.at[n],
@@ -265,8 +481,7 @@
             return c
 
         if n == 0:
-            w1_load(0).wait()
-            w1_load(1).wait()
+            w1_load.wait()
         lax.fori_loop(0, width // 512, hidden, 0)
         if n < 2:
             x_load(n + 2).start()
@@ -304,61 +519,36 @@
     y_ref[...] = (part[0] + near[0] + near[1]).astype(BF)
 
 
-def mlp(x_loc, normed, wide, oin, w1, w2, wo, side):
+def mlp(x_loc, normed, wide, oin, own, full, cores, side):
     rows, model = normed.shape
-    width = w1.shape[0]
+    groups = side * cores
+    width, heads = groups * own[0].shape[0], groups * own[2].shape[0]
     anywhere = pl.BlockSpec(memory_space=pl.ANY)
-    flops = 2 * side * rows * model * (2 * width + wo.shape[0])
+    flops = 2 * side * rows * model * (2 * width + heads)
     return pl.pallas_call(
-        functools.partial(mlp_kernel, side),
-        in_specs=[anywhere] * 7,
+        functools.partial(mlp_kernel, side, cores),
+        in_specs=[anywhere] * 10,
         out_specs=pl.BlockSpec(memory_space=pltpu.VMEM),
         out_shape=jax.ShapeDtypeStruct((rows, model), BF),
         scratch_shapes=[
-            pltpu.VMEM(w1.shape, BF),
-            pltpu.VMEM((width + wo.shape[0], model), BF),
+            pltpu.VMEM((width, model), BF),
+            pltpu.VMEM((width + heads, model), BF),
             pltpu.VMEM((2, rows, model), BF),
             pltpu.VMEM((model, rows), BF),
             pltpu.VMEM(oin.shape, BF),
-            pltpu.VMEM((rows, width + wo.shape[0]), BF),
+            pltpu.VMEM((rows, width + heads), BF),
             pltpu.VMEM((3, rows, model), F32),
             pltpu.VMEM((2, rows // 2, model), F32),
             pltpu.VMEM((2, rows, model), F32),
             pltpu.VMEM((rows, model), BF),
-            pltpu.SemaphoreType.DMA((8,)),
+            pltpu.SemaphoreType.DMA((7,)),
             pltpu.SemaphoreType.DMA((6,)),
             pltpu.SemaphoreType.DMA((6,)),
         ],
         compiler_params=pltpu.CompilerParams(vmem_limit_bytes=62 * 1024 * 1024, collective_id=2, has_side_effects=True),
         cost_estimate=pl.CostEstimate(flops=flops, bytes_accessed=4 * model * width, transcendentals=side * rows * width),
         name="mlp",
-    )(normed, wide, oin, w1, w2, wo, x_loc)
-
-
-def layer_norm(row_vals, ln_gain):
-    row_mean = jnp.mean(row_vals, axis=-1, keepdims=True)
-    centered = row_vals - row_mean
-    row_var = jnp.mean(centered * centered, axis=-1, keepdims=True)
-    return (centered * lax.rsqrt(row_var + LN_EPS) * ln_gain).astype(BF)
-
-
-def ring_gather(block, axis, side):
-    up = [(j, (j + 1) % side) for j in range(side)]
-    down = [(j, (j - 1) % side) for j in range(side)]
-    rows = block.shape[0]
-    half = rows // 2
-    before = lax.ppermute(block, axis, up)
-    after = lax.ppermute(block, axis, down)
-    far_a = lax.ppermute(before[:half], axis, up)
-    far_b = lax.ppermute(after[half:], axis, down)
-    me = lax.axis_index(axis)
-    full = jnp.zeros((side * rows, block.shape[1]), block.dtype)
-    place = lambda full, part, pos, off: lax.dynamic_update_slice(full, part, (pos % side * rows + off, 0))
-    full = place(full, block, me, 0)
-    full = place(full, before, me - 1 + side, 0)
-    full = place(full, after, me + 1, 0)
-    full = place(full, far_a, me + 2, 0)
-    return place(full, far_b, me + 2, half)
+    )(normed, wide, oin, *own, *full, x_loc)
 
 
 def solution(mesh):
@@ -366,20 +556,12 @@
     side = math.isqrt(tp // 2)
     cores = tp // (side * side)
     grid = Mesh(mesh.devices.reshape(data, side, side, cores), ("data", "y", "x", "core"))
-    row, col = ("x", "core"), ("y", "core")
 
     def local_block(x_loc, ln_gamma, w_qkv, w_out, w_up, w_down):
-        normed = layer_norm(x_loc.astype(F32), ln_gamma)
-        wqkv = lax.all_gather(w_qkv[:, 0, :].T, row, axis=0, tiled=True)
-        tall = ring_gather(normed, "y", side)
-        qkv = lax.dot_general(wqkv, tall, (((1,), (1,)), ((), ())), preferred_element_type=F32).astype(BF)
-        qkv = qkv.reshape(side * cores, -1, tall.shape[0])
-        qkv = lax.all_to_all(qkv, row, split_axis=0, concat_axis=0, tiled=True)
-        oin, wide = attention(qkv, normed, cores, side)
-        wup = lax.all_gather(w_up.T, col, axis=0, tiled=True)
-        wout = lax.all_gather(w_out[0], col, axis=0, tiled=True)
-        wdown = lax.all_gather(w_down, col, axis=0, tiled=True)
-        return mlp(x_loc, normed, wide, oin, wup, wdown, wout, side)
+        own = (w_up.T, w_down, w_out[0])
+        qkv, normed, w1 = qkv_stage(x_loc, ln_gamma[None], w_qkv[:, 0, :].T, own[0], cores, side)
+        oin, wide, w2, wo = attention(qkv, normed, own[1], own[2], cores, side)
+        return mlp(x_loc, normed, wide, oin, own, (w1, w2, wo), cores, side)
 
     row_spec = P(("data", "y", "x", "core"), None)
     tp_axes = ("y", "x", "core")

time: 359 us -> 362 us (level)
  Pallas kernels: 191 us -> 353 us
  waiting for transfers between devices: 59.9 us -> 0 us
  blocking collectives: 52 us -> 0 us
  matrix products: 16.5 us -> 0 us
  between operations: 13.3 us -> 0.04 us
  starting transfers between devices: 8.21 us -> 0 us
  local copies, waits for them, and re-layouts: 15.6 us -> 8.25 us
    pallas_call x1 -> x2, Pallas kernels: 105 us -> 238 us  [the longest x1 139 us: qkv_stage(): pl.pallas_call(functools.partial(qkv_kernel, side, cores), in_specs=[vmem...]
    all_to_all x1 -> x0, blocking collectives: 52 us -> none  [local_block(): qkv = lax.all_to_all(qkv, row, split_axis=0, concat_axis=0, tiled=True)]
    ppermute x4 -> x0, waiting for transfers between devices: 40 us -> none  [the longest x1 28.6 us: ring_gather(): before = lax.ppermute(block, axis, up)]
    pallas_call x1, Pallas kernels: 86.1 us -> 115 us  [attention(): pl.pallas_call(functools.partial(attn_kernel, hd, side, cores, toks // si...]
    all_gather x4 -> x0, waiting for transfers between devices: 17.1 us -> none  [the longest x1 17.1 us: local_block(): wup = lax.all_gather(w_up.T, col, axis=0, tiled=True)]
    dot_general x1 -> x0, matrix products: 16.5 us -> none  [local_block(): lax.dot_general(wqkv, tall, (((1,), (1,)), ((), ())), preferred_element_t...]
    ppermute x4 -> x0, starting transfers between devices: 8.03 us -> none  [the longest x1 2.73 us: ring_gather(): far_b = lax.ppermute(after[half:], axis, down)]
    convert_element_type x1 -> x0, local copies, waits for them, and re-layouts: 6.35 us -> none  [local_block(): lax.dot_general(wqkv, tall, (((1,), (1,)), ((), ())), preferred_element_t...]
  transfers between devices with their start and end apart: 8 -> 0, of which waited for: 3 -> 0; matrix products, arithmetic and copies ran while one was open for 8% -> 0% of each run, Pallas kernels for 24% -> 0%
where the time goes in v4:
time: 362 us; the launch traced here: 361 us
  Pallas kernels  353 us (98%)
  local copies, waits for them, and re-layouts  8.25 us (2%)
    pallas_call x1, Pallas kernels, qkv_stage(): pl.pallas_call(functools.partial(qkv_kernel, side, cores), in_specs=[vmem...  139 us
    pallas_call x1, Pallas kernels, attention(): pl.pallas_call(functools.partial(attn_kernel, hd, side, cores, toks // si...  115 us
    pallas_call x1, Pallas kernels, mlp(): pl.pallas_call(functools.partial(mlp_kernel, side, cores), in_specs=[anyw...  99.5 us
    unnamed x9, local copies, waits for them, and re-layouts  7.54 us

profile of v4, /device:TPU:97, one launch (start us, length us, event | category | flops | bytes accessed | tf_op | source)
XLA Modules:
  0.0 361.2 jit_solution(6729613681912410540)
XLA Ops:
  0.0 0.7 broadcast_in_dim.3.gain_ref
  0.7 0.0 copy-start
  0.7 1.4 copy-done
  2.1 0.0 copy-start.1
  2.1 1.3 copy-done.1
  3.5 0.0 copy-start.2
  3.5 1.3 copy-done.2
  4.8 138.8 %qkv.1 = (bf16[8,240,1024]{2,1,0:T(8,128)(2,1)}, bf16[256,2560]{1,0:T(8,128)(2,1)S(1)}, bf16[8,320,2560]{2,1,0:T(8,128)(2,1)}) custom-call(bf16[256,2560]{1,0:T(8,128)(2,1)S(1)} %copy-done.1, f32[1,2560]{1,0:T(1,128)S(1)} %broadcast_in_dim.3.gain_ref, bf16[240,2560]{1,0:T(8,128)(2,1)S(1)} %bitcast.7, bf16[320,2560]{1,0:T(8,128)(2,1)S(1)} %bitcast.6), custom_call_target="tpu_custom_call" | custom-call | flops 10066329600 | bytes 3276800 | tf_op jit(solution)/shard_map/qkv/pallas_call | solution.py:194
  143.6 0.0 copy-start.3
  143.6 1.0 copy-done.3
  144.6 114.6 %attention.1 = (bf16[8,80,1024]{2,1,0:T(8,128)(2,1)}, bf16[4,256,2560]{2,1,0:T(8,128)(2,1)}, bf16[8,320,2560]{2,1,0:T(8,128)(2,1)}, bf16[8,80,2560]{2,1,0:T(8,128)(2,1)}) custom-call(bf16[8,240,1024]{2,1,0:T(8,128)(2,1)} %get-tuple-element.13.qkv_ref, bf16[256,2560]{1,0:T(8,128)(2,1)} %copy-done.3, bf16[320,2560]{1,0:T(8,128)(2,1)} %w2_own.1, ...), custom_call_target="tpu_custom_call" | custom-call | flops 32212254720 | bytes 5242880 | tf_op jit(solution)/shard_map/attention/pallas_call | solution.py:378
  259.2 99.5 %mlp.1 = bf16[256,2560]{1,0:T(8,128)(2,1)} custom-call(bf16[256,2560]{1,0:T(8,128)(2,1)} %copy-done.3, bf16[4,256,2560]{2,1,0:T(8,128)(2,1)} %get-tuple-element.14.wide_ref, bf16[8,80,1024]{2,1,0:T(8,128)(2,1)} %get-tuple-element.15.oin_ref, bf16[320,2560]{1,0:T(8,128)(2,1)} %bitcast.5, bf16[320,2560]{1,0:T(8,128)(2,1)} %w2_own.1, bf16[80,2560]{1,0:T(8,128)(2,1)} %bitcast.9, ...), custom_call_target="tpu_custom_call" | custom-call | flops 30198988800 | bytes 26214400 | tf_op jit(solution)/shard_map/mlp/pallas_call | solution.py:528
  358.8 2.5 copy.8
Async XLA Ops:
  0.7 1.4 copy-start
  2.1 1.3 copy-start.1
  3.5 1.3 copy-start.2
  143.6 1.1 copy-start.3

commit v5 on v4

--- a/solution.py
+++ b/solution.py
@@ -16,11 +16,11 @@
 ROWS = 64
 
 
-def ring(own, full, axis, split, send, recv):
+def ring(own, slot, axis, split, send, recv):
     side, cores = lax.axis_size(axis), lax.axis_size("core")
     at, core = lax.axis_index(axis), lax.axis_index("core")
     other = (core + 1) % cores
-    block = lambda hop: full.at[(at + hop) % side * cores + core]
+    block = lambda hop: slot((at + hop) % side * cores + core)
     head, tail = pl.ds(0, split), pl.ds(split, own.shape[0] - split)
     nxt, prv, sib = {axis: (at + 1) % side}, {axis: (at + side - 1) % side}, {"core": other}
     plan = (
@@ -67,8 +67,8 @@
     meet(up, down, *[
         {"x": (x + dx) % side, "core": (core + dc) % cores} for dx in range(side) for dc in range(cores) if dx or dc])
 
-    wq = ring(wq_ref, wv, "x", wq_ref.shape[0] // 32 * 16, wq_send, wq_recv)
-    w1 = ring(w1_ref, w1_full, "y", w1_ref.shape[0] // 2, w1_send, w1_recv)
+    wq = ring(wq_ref, lambda n: wv.at[n], "x", wq_ref.shape[0] // 32 * 16, wq_send, wq_recv)
+    w1 = ring(w1_ref, lambda n: w1_full.at[n], "y", w1_ref.shape[0] // 2, w1_send, w1_recv)
     own_wq = pltpu.make_async_copy(wq_ref, wv.at[me], local.at[0])
     own_wq.start()
     start(wq, 0, 1, 2)
@@ -109,7 +109,7 @@
 
     flip(y)
     start(xs, 0, 1)
-    start(w1, 2, 0, 1)
+    start(w1, 2)
     keep = pltpu.make_async_copy(xv.at[y], normed_ref, local.at[1])
     keep.start()
 
@@ -128,6 +128,7 @@
     start(wq, 3, 4, 5, 6)
     arrived(xs, 0, 1)
     start(xs, 2, 3)
+    start(w1, 0, 1)
     flip(before)
     flip(after)
     own_wq.wait()
@@ -207,7 +208,7 @@
             pltpu.VMEM((groups, wq.shape[0], side * rows), BF),
             dma(8), dma(8), dma(4), dma(4), dma(8), dma(8), dma(groups), dma(groups), dma(3),
         ],
-        compiler_params=pltpu.CompilerParams(vmem_limit_bytes=48 * 1024 * 1024, collective_id=0, has_side_effects=True),
+        compiler_params=pltpu.CompilerParams(vmem_limit_bytes=58 * 1024 * 1024, collective_id=0, has_side_effects=True),
         cost_estimate=pl.CostEstimate(flops=2 * side * rows * model * groups * wq.shape[0], bytes_accessed=4 * w1.size, transcendentals=0),
         name="qkv",
     )(x_loc, gain, wq, w1)
@@ -242,8 +243,8 @@
             src_ref=o_buf.at[step % 2], dst_ref=oin_ref.at[me], send_sem=o_send.at[step % 2], recv_sem=o_recv.at[step],
             device_id={"y": to // cores, "core": to % cores}, device_id_type=MESH)
 
-    w2 = ring(w2_ref, w2_full, "y", w2_ref.shape[0] // 2, w2_send, w2_recv)
-    wo = ring(wo_ref, wo_full, "y", wo_ref.shape[0] // 32 * 16, wo_send, wo_recv)
+    w2 = ring(w2_ref.at[:, pl.ds(0, w2_full.shape[2])], lambda n: w2_full.at[n], "y", w2_ref.shape[0] // 2, w2_send, w2_recv)
+    wo = ring(wo_ref, lambda n: wo_full.at[n], "y", wo_ref.shape[0] // 32 * 16, wo_send, wo_recv)
 
     def load_query(b, slot):
         b = jnp.minimum(b, 2 * groups - 1)
@@ -369,6 +370,10 @@
                 copy.wait_send()
 
 
+def first_columns(model):
+    return model * 2 // 5 // 256 * 256
+
+
 def attention(qkv, normed, w2, wo, cores, side):
     groups, three, toks = qkv.shape
     hd = three // 3
@@ -383,7 +388,7 @@
         out_shape=[
             jax.ShapeDtypeStruct((groups, hd, toks), BF),
             jax.ShapeDtypeStruct((side,) + normed.shape, BF),
-            jax.ShapeDtypeStruct((groups,) + w2.shape, BF),
+            jax.ShapeDtypeStruct((groups, w2.shape[0], first_columns(w2.shape[1])), BF),
             jax.ShapeDtypeStruct((groups,) + wo.shape, BF),
         ],
         scratch_shapes=[
@@ -410,15 +415,17 @@
 
 
 def mlp_kernel(side, cores, x_ref, wide_ref, oin_ref, w1_own, w2_own, wo_own, w1_ref, w2_ref, wo_ref, res_ref, y_ref, w1, w2, xv, xt, ov,
-               hv, part, far, near, res, load, send, recv):
-    x = lax.axis_index("x")
-    right, left = (x + 1) % side, (x + side - 1) % side
+               hv, part, far, near, res, load, send, recv, w2_send, w2_recv):
+    x, y = lax.axis_index("x"), lax.axis_index("y")
+    right, left = {"x": (x + 1) % side}, {"x": (x + side - 1) % side}
     rows, model = x_ref.shape
     groups = w1_ref.shape[0]
     width = groups * w1_own.shape[0]
     heads = groups * wo_own.shape[0]
+    cut = w2_ref.shape[2]
+    step = math.gcd(cut, model - cut, 512)
     half = rows // 2
-    me = lax.axis_index("y") * cores + lax.axis_index("core")
+    me = y * cores + lax.axis_index("core")
     top, low = pl.ds(0, half), pl.ds(half, half)
     order = (2, 1, 3, 0)
 
@@ -426,40 +433,34 @@
         src = x_ref if order[n] == 0 else wide_ref.at[order[n]]
         return pltpu.make_async_copy(src, xv.at[n % 2], load.at[n % 2])
 
+    def shard(into, base, size, n, columns):
+        return into.at[pl.ds(pl.multiple_of(base + n * size, 16), size), columns]
+
     def gathered(own, full, into, base, sem):
-        size = own.shape[0]
+        size, columns = full.shape[1], pl.ds(0, full.shape[2])
         for hop in range(groups):
-            slot = (me + hop) % groups
-            to = into.at[pl.ds(pl.multiple_of(base + slot * size, 16), size)]
-            pltpu.make_async_copy(full.at[slot] if hop else own, to, sem).start()
-        whole = into.at[pl.ds(base, groups * size)]
+            n = (me + hop) % groups
+            pltpu.make_async_copy(full.at[n] if hop else own.at[:, columns], shard(into, base, size, n, columns), sem).start()
+        whole = into.at[pl.ds(base, groups * size), columns]
         return pltpu.make_async_copy(whole, whole, sem)
 
     o_load = pltpu.make_async_copy(oin_ref, ov, load.at[2])
     res_load = pltpu.make_async_copy(res_ref, res, load.at[3])
+    rest = pl.ds(cut, model - cut)
+    rest_own = pltpu.make_async_copy(w2_own.at[:, rest], shard(w2, 0, width // groups, me, rest), load.at[7])
     x_load(0).start()
     w1_load = gathered(w1_own, w1_ref, w1, 0, load.at[4])
     o_load.start()
     w2_load = gathered(w2_own, w2_ref, w2, 0, load.at[5])
     wo_load = gathered(wo_own, wo_ref, w2, width, load.at[6])
+    rest_own.start()
     x_load(1).start()
     res_load.start()
-    meet({"x": right}, {"x": left})
-
-    def put(n, src, dst, to):
-        return pltpu.make_async_remote_copy(src_ref=src, dst_ref=dst, send_sem=send.at[n], recv_sem=recv.at[n],
-                                            device_id={"x": to}, device_id_type=MESH)
-
-    puts = (
-        put(0, part.at[0, top], far.at[0], right),
-        put(1, part.at[0, low], far.at[1], left),
-        put(2, part.at[1, low], near.at[0, low], right),
-        put(3, part.at[2, top], near.at[1, top], left),
-        put(4, part.at[1, top], near.at[0, top], right),
-        put(5, part.at[2, low], near.at[1, low], left),
-    )
-
-    def compute(n, slot):
+    meet(right, left, {"y": (y + 1) % side}, {"y": (y + side - 1) % side}, {"core": (lax.axis_index("core") + 1) % cores})
+    w2_rest = ring(w2_own.at[:, rest], lambda n: shard(w2, 0, width // groups, n, rest), "y", width // groups // 2, w2_send, w2_recv)
+    start(w2_rest, 0, 1, 2)
+
+    def hidden(n):
         x_load(n).wait()
 
         def flip(k, c):
@@ -468,54 +469,88 @@
             return c
 
         lax.fori_loop(0, model // 256, flip, 0, unroll=2)
-        hd, toks = ov.shape[1:]
+        if n < 2:
+            x_load(n + 2).start()
         col = pl.multiple_of((x + order[n]) % side * rows, rows)
         if n == 0:
             o_load.wait()
-        hv[:, width:] = ov[:, :, pl.ds(col, rows)].reshape(heads, rows).T
-
-        def hidden(f, c):
+        hv[n, :, width:] = ov[:, :, pl.ds(col, rows)].reshape(heads, rows).T
+        if n == 0:
+            w1_load.wait()
+
+        def piece(f, c):
             at = pl.ds(pl.multiple_of(f * 512, 512), 512)
             pre = jnp.dot(w1[at, :], xt[...], preferred_element_type=F32)
-            hv[:, at] = jax.nn.gelu(pre, approximate=True).astype(BF).T
+            hv[n, :, at] = jax.nn.gelu(pre, approximate=True).astype(BF).T
             return c
 
-        if n == 0:
-            w1_load.wait()
-        lax.fori_loop(0, width // 512, hidden, 0)
-        if n < 2:
-            x_load(n + 2).start()
+        lax.fori_loop(0, width // 512, piece, 0)
+
+    def outs(n, lo, hi):
+        def piece(d, c):
+            at = pl.ds(pl.multiple_of(d * step, step), step)
+            part[n % 3, :, at] = jnp.dot(hv[n], w2[:, at], preferred_element_type=F32)
+            return c
+
+        lax.fori_loop(lo // step, hi // step, piece, 0)
+
+    def phase(lo, hi, first, prepare, between):
+        cols = pl.ds(lo, hi - lo)
+        plan = (
+            (part.at[0, top, cols], far.at[0, :, cols], right),
+            (part.at[0, low, cols], far.at[1, :, cols], left),
+            (part.at[1, low, cols], near.at[0, low, cols], right),
+            (part.at[2, top, cols], near.at[1, top, cols], left),
+            (part.at[1, top, cols], near.at[0, top, cols], right),
+            (part.at[2, low, cols], near.at[1, low, cols], left),
+        )
+        puts = [
+            pltpu.make_async_remote_copy(src_ref=src, dst_ref=dst, send_sem=send.at[first + n], recv_sem=recv.at[first + n],
+                                         device_id=to, device_id_type=MESH)
+            for n, (src, dst, to) in enumerate(plan)
+        ]
+        prepare(0)
+        outs(0, lo, hi)
+        start(puts, 0, 1)
+        prepare(1)
+        outs(1, lo, hi)
+        start(puts, 2)
+        prepare(2)
+        outs(2, lo, hi)
+        start(puts, 3)
+        between()
+        puts[0].wait()
+        part[1, :half, lo:hi] += far[0, :, lo:hi]
+        start(puts, 4)
+        puts[1].wait()
+        part[2, half:, lo:hi] += far[1, :, lo:hi]
+        start(puts, 5)
+        prepare(3)
+        outs(3, lo, hi)
+        return puts[2:]
+
+    def ready(n):
+        hidden(n)
         if n == 0:
             w2_load.wait()
             wo_load.wait()
 
-        def outs(d, c):
-            at = pl.ds(pl.multiple_of(d * 512, 512), 512)
-            part[slot, :, at] = jnp.dot(hv[...], w2[:, at], preferred_element_type=F32)
-            return c
-
-        lax.fori_loop(0, model // 512, outs, 0)
-
-    compute(0, 0)
-    puts[0].start()
-    puts[1].start()
-    compute(1, 1)
-    puts[2].start()
-    compute(2, 2)
-    puts[3].start()
-    puts[0].wait()
-    part[1, :half, :] += far[0]
-    puts[4].start()
-    puts[1].wait()
-    part[2, half:, :] += far[1]
-    puts[5].start()
-    compute(3, 0)
+    def pass_on():
+        arrived(w2_rest, 0, 1)
+        start(w2_rest, 3, 4, 5, 6)
+
+    waits = phase(0, cut, 0, ready, pass_on)
+    arrived(w2_rest, 3, 4)
+    start(w2_rest, 7)
+    rest_own.wait()
+    arrived(w2_rest, 2, 5, 6, 7)
+    waits += phase(cut, model, 6, lambda n: None, lambda: None)
     res_load.wait()
     part[0] += res[...].astype(F32)
-    puts[2].wait()
-    puts[3].wait()
-    puts[4].wait()
-    puts[5].wait()
+    for put in waits:
+        put.wait()
+    for copy in w2_rest:
+        copy.wait_send()
     y_ref[...] = (part[0] + near[0] + near[1]).astype(BF)
 
 
@@ -536,16 +571,18 @@
             pltpu.VMEM((2, rows, model), BF),
             pltpu.VMEM((model, rows), BF),
             pltpu.VMEM(oin.shape, BF),
-            pltpu.VMEM((rows, width + heads), BF),
+            pltpu.VMEM((side, rows, width + heads), BF),
             pltpu.VMEM((3, rows, model), F32),
             pltpu.VMEM((2, rows // 2, model), F32),
             pltpu.VMEM((2, rows, model), F32),
             pltpu.VMEM((rows, model), BF),
-            pltpu.SemaphoreType.DMA((7,)),
-            pltpu.SemaphoreType.DMA((6,)),
-            pltpu.SemaphoreType.DMA((6,)),
+            pltpu.SemaphoreType.DMA((8,)),
+            pltpu.SemaphoreType.DMA((12,)),
+            pltpu.SemaphoreType.DMA((12,)),
+            pltpu.SemaphoreType.DMA((8,)),
+            pltpu.SemaphoreType.DMA((8,)),
         ],
-        compiler_params=pltpu.CompilerParams(vmem_limit_bytes=62 * 1024 * 1024, collective_id=2, has_side_effects=True),
+        compiler_params=pltpu.CompilerParams(vmem_limit_bytes=67043328, collective_id=2, has_side_effects=True),
         cost_estimate=pl.CostEstimate(flops=flops, bytes_accessed=4 * model * width, transcendentals=side * rows * width),
         name="mlp",
     )(normed, wide, oin, *own, *full, x_loc)

time: 362 us -> 310 us (0.86)
  Pallas kernels: 353 us -> 306 us
  local copies, waits for them, and re-layouts: 8.25 us -> 3.77 us
    pallas_call x1, Pallas kernels: 115 us -> 86.3 us  [attention(): pl.pallas_call(functools.partial(attn_kernel, hd, side, cores, toks // si...]
    pallas_call x1, Pallas kernels: 139 us -> 116 us  [qkv_stage(): pl.pallas_call(functools.partial(qkv_kernel, side, cores), in_specs=[vmem...]
    unnamed x9 -> x1, local copies, waits for them, and re-layouts: 7.54 us -> 2.46 us
    pallas_call x1, Pallas kernels: 99.5 us -> 104 us  [mlp(): pl.pallas_call(functools.partial(mlp_kernel, side, cores), in_specs=[anyw...]
where the time goes in v5:
time: 310 us
  Pallas kernels  306 us (99%)
  local copies, waits for them, and re-layouts  3.77 us (1%)
    pallas_call x1, Pallas kernels, qkv_stage(): pl.pallas_call(functools.partial(qkv_kernel, side, cores), in_specs=[vmem...  116 us
    pallas_call x1, Pallas kernels, mlp(): pl.pallas_call(functools.partial(mlp_kernel, side, cores), in_specs=[anyw...  104 us
    pallas_call x1, Pallas kernels, attention(): pl.pallas_call(functools.partial(attn_kernel, hd, side, cores, toks // si...  86.3 us

profile of v5, /device:TPU:97, one launch (start us, length us, event | category | flops | bytes accessed | tf_op | source)
XLA Modules:
  0.0 309.8 jit_solution(17586342628265645780)
XLA Ops:
  0.0 1.3 broadcast_in_dim.3.gain_ref
  1.3 116.1 %qkv.1 = (bf16[8,240,1024]{2,1,0:T(8,128)(2,1)}, bf16[256,2560]{1,0:T(8,128)(2,1)}, bf16[8,320,2560]{2,1,0:T(8,128)(2,1)}) custom-call(bf16[256,2560]{1,0:T(8,128)(2,1)} %res_ref.1, f32[1,2560]{1,0:T(1,128)} %broadcast_in_dim.3.gain_ref, bf16[240,2560]{1,0:T(8,128)(2,1)} %bitcast.7, bf16[320,2560]{1,0:T(8,128)(2,1)} %bitcast.5), custom_call_target="tpu_custom_call" | custom-call | flops 10066329600 | bytes 3276800 | tf_op jit(solution)/shard_map/qkv/pallas_call | solution.py:195
  117.4 86.3 %attention.1 = (bf16[8,80,1024]{2,1,0:T(8,128)(2,1)}, bf16[4,256,2560]{2,1,0:T(8,128)(2,1)}, bf16[8,320,1024]{2,1,0:T(8,128)(2,1)}, bf16[8,80,2560]{2,1,0:T(8,128)(2,1)}) custom-call(bf16[8,240,1024]{2,1,0:T(8,128)(2,1)} %get-tuple-element.13.qkv_ref, bf16[256,2560]{1,0:T(8,128)(2,1)} %get-tuple-element.12.x_ref, bf16[320,2560]{1,0:T(8,128)(2,1)} %w2_own.1, ...), custom_call_target="tpu_custom_call" | custom-call | flops 32212254720 | bytes 5242880 | tf_op jit(solution)/shard_map/attention/pallas_call | solution.py:383
  203.8 103.6 %mlp.1 = bf16[256,2560]{1,0:T(8,128)(2,1)} custom-call(bf16[256,2560]{1,0:T(8,128)(2,1)} %get-tuple-element.12.x_ref, bf16[4,256,2560]{2,1,0:T(8,128)(2,1)} %get-tuple-element.14.wide_ref, bf16[8,80,1024]{2,1,0:T(8,128)(2,1)} %get-tuple-element.15.oin_ref, bf16[320,2560]{1,0:T(8,128)(2,1)} %bitcast.6, bf16[320,2560]{1,0:T(8,128)(2,1)} %w2_own.1, ...), custom_call_target="tpu_custom_call" | custom-call | flops 30198988800 | bytes 26214400 | tf_op jit(solution)/shard_map/mlp/pallas_call | solution.py:563
  307.3 2.5 copy.8
